TPU v7x, 8 devices: a whole 2x2x1 slice. The times are simulated.
8 devices in a mesh: dp: 2 (over z, y), cp: 4 (over x, core).
Axes of the slice: x: 2, y: 2, z: 1, core: 2. Of those that a mesh axis runs over, the one named last changes fastest.
Arguments:
- queries: bfloat16 [64, 512, 10, 256], P('dp', 'cp'), parts along dimension 0
- key_states: bfloat16 [64, 512, 256], P('dp', 'cp'), parts along dimension 0
- value_states: bfloat16 [64, 512, 256], P('dp', 'cp'), parts along dimension 0
- segment_ids: int32 [64, 512], P('dp', 'cp'), parts along dimension 0
Outputs:
- output 1: bfloat16 [64, 512, 10, 256], P('dp', 'cp'), parts along dimension 0
- output 2: float32 [64, 512, 10], P('dp', 'cp'), parts along dimension 0
There are 2 independent parts. A program takes and returns all parts, laid end to end along the dimension named above; each array names one.
All inputs are finite; a program needn't handle non-finite values.
Results may differ from a plain program's by a relative error of at most 0.00326493.
Values are sent between devices in bfloat16 or wider.
A program may use at most 1 GiB of HBM per device.

v0:
```python
import functools

import jax
import jax.numpy as jnp
from jax import lax
from jax.experimental import pallas as pl
from jax.experimental.pallas import tpu as pltpu
from jax.sharding import PartitionSpec as P


CHUNKS = (6, 6, 5, 5, 5, 5)
BOUNDS = tuple(sum(CHUNKS[:n]) for n in range(len(CHUNKS) + 1))
GROUP = 2
DEPTH = 3
LOG2E = 1.4426950408889634

ACROSS = [(0, 2), (1, 3)]
BESIDE = [(0, 1), (2, 3)]
SWAP = [(2, 3), (3, 2)]


def pack_kernel(ranges, tails, seg_ref, k_ref, v_ref, *rest):
    outs, (seg_scr, seg_sem, sem) = rest[:-3], rest[-3:]
    batch, piece, head = k_ref.shape
    segments = pltpu.make_async_copy(seg_ref, seg_scr, seg_sem)
    segments.start()

    def copies(i, out, at):
        for half, ref in enumerate((k_ref, v_ref)):
            rows = pl.ds(pl.multiple_of((2 * i + half) * piece, piece), piece)
            yield pltpu.make_async_copy(ref.at[at + i], out.at[rows], sem)

    for out, (a, b) in zip(outs, ranges):
        @pl.loop(0, b - a)
        def _(i):
            for copy in copies(i, out, a):
                copy.start()
    segments.wait()
    here = jnp.sum((seg_scr[...] == 0).astype(jnp.float32), axis=1, keepdims=True)
    rows = jnp.broadcast_to(here, (batch, head)).astype(jnp.bfloat16)
    for out, (a, b), tail in zip(outs, ranges, tails):
        if tail:
            out[(b - a) * 2 * piece:] = rows
    for out, (a, b) in zip(outs, ranges):
        @pl.loop(0, b - a)
        def _(i):
            for copy in copies(i, out, a):
                copy.wait()


def pack(ranges, tails, seg, k, v):
    batch, piece, head = k.shape
    vmem, hbm = pl.BlockSpec(memory_space=pltpu.VMEM), pl.BlockSpec(memory_space=pltpu.HBM)
    seg, k, v = (pltpu.with_memory_space_constraint(x, pltpu.HBM) for x in (seg, k, v))
    return pl.pallas_call(
        functools.partial(pack_kernel, ranges, tails),
        in_specs=[hbm] * 3,
        out_specs=[vmem] * len(ranges),
        out_shape=[
            jax.ShapeDtypeStruct(((b - a) * 2 * piece + (batch if tail else 0), head), jnp.bfloat16)
            for (a, b), tail in zip(ranges, tails)
        ],
        scratch_shapes=[pltpu.VMEM(seg.shape, jnp.int32), pltpu.SemaphoreType.DMA, pltpu.SemaphoreType.DMA],
        compiler_params=pltpu.CompilerParams(vmem_limit_bytes=16 << 20),
        cost_estimate=pl.CostEstimate(flops=1 << 20, bytes_accessed=4 * k.size, transcendentals=0),
    )(seg, k, v)


def attend_kernel(first, last, base, size, s_hbm, cut_ref, q_ref, k_ref, v_ref, near_ref, fara_ref, farb_ref, *rest):
    if not first:
        _, lse_in, q_in, kv_in, *rest = rest
    o_ref, lse_ref, *rest = rest
    if not last:
        q_out, kv_out, *rest = rest
    s_ref, n_ref, q_buf, k_buf, v_buf, o_buf, s_sem, kv_sem, q_sem, o_sem, ahead_sem = rest
    depth, heads, piece, head = q_buf.shape
    batch = lse_ref.shape[1]
    groups = heads // GROUP
    width = GROUP * piece
    scale = head ** -0.5
    me = lax.axis_index("cp")
    odd = lax.rem(me, 2)
    scalars = pltpu.make_async_copy(s_hbm, s_ref, s_sem)
    scalars.start()

    def kv_loads(step):
        slot = lax.rem(step, depth)
        seq = base + step
        there = pl.ds(pl.multiple_of(jnp.where(odd == 1, 1, 3) * piece, piece), piece)
        out = []
        for half, (ref, buf) in enumerate(((k_ref, k_buf), (v_ref, v_buf))):
            rows = pl.ds(pl.multiple_of((2 * seq + half) * piece, piece), piece)
            out.append(pltpu.make_async_copy(ref.at[seq], buf.at[slot, pl.ds(0, piece)], kv_sem.at[slot]))
            out.append(pltpu.make_async_copy(near_ref.at[rows], buf.at[slot, there], kv_sem.at[slot]))
        return out

    def aheads():
        at = base + size
        out = [pltpu.make_async_copy(q_ref.at[at], q_out, ahead_sem)]
        for half, ref in enumerate((k_ref, v_ref)):
            near_rows = pl.ds((2 * at + half) * piece, piece)
            out.append(pltpu.make_async_copy(ref.at[at], kv_out.at[2 * half], ahead_sem))
            out.append(pltpu.make_async_copy(near_ref.at[near_rows], kv_out.at[2 * half + 1], ahead_sem))
        return out

    def part(g):
        return pl.ds(g * GROUP, GROUP)

    def q_load(step, g):
        slot = lax.rem(step, depth)
        return pltpu.make_async_copy(q_ref.at[base + step, part(g)], q_buf.at[slot, part(g)], q_sem.at[slot, g])

    def o_store(step, g):
        slot = lax.rem(step, 2)
        return pltpu.make_async_copy(o_buf.at[slot, part(g)], o_ref.at[base + step, part(g)], o_sem.at[slot, g])

    def load(step):
        for copy in kv_loads(step):
            copy.start()
        for g in range(groups):
            q_load(step, g).start()

    def place(step):
        slot = lax.rem(step, depth)
        for ref, block in ((fara_ref, 2), (farb_ref, jnp.where(odd == 1, 3, 1))):
            there = pl.ds(pl.multiple_of(block * piece, piece), piece)
            for half, buf in enumerate((k_buf, v_buf)):
                buf[slot, there] = ref[pl.ds(pl.multiple_of((2 * step + half) * piece, piece), piece)]

    def run(count, step, cut):
        seq = base + step
        slot, out = lax.rem(step, depth), lax.rem(step, 2)
        keys = count * piece
        lane = lax.broadcasted_iota(jnp.int32, (piece, piece), 1)
        row = lax.broadcasted_iota(jnp.int32, (piece, piece), 0)
        low = jnp.maximum(jnp.where(row >= cut, cut, -keys), -me * piece)
        caps = [
            jnp.where((lane - n * piece <= row) & (lane - n * piece >= low), jnp.inf, -jnp.inf) for n in range(count)
        ]
        cap = jnp.concatenate([jnp.concatenate(caps, axis=1)] * GROUP, axis=0)
        logs = jnp.zeros((piece, piece), jnp.float32)

        def scores(g):
            q = q_buf[slot, g * GROUP:(g + 1) * GROUP].reshape(width, head)
            s = lax.dot_general(q, k_buf[slot, :keys], (((1,), (1,)), ((), ())), preferred_element_type=jnp.float32)
            s = jnp.minimum(s, cap)
            return s, jnp.max(s, axis=1, keepdims=True)

        def weigh(s, m):
            p = jnp.exp2((s - m) * (scale * LOG2E))
            return p.astype(jnp.bfloat16), m, jnp.sum(p, axis=1, keepdims=True)

        def finish(g, logs, p, m, l):
            o = jnp.dot(p, v_buf[slot, :keys], preferred_element_type=jnp.float32) * (1.0 / l)
            o_buf[out, g * GROUP:(g + 1) * GROUP] = o.astype(jnp.bfloat16).reshape(GROUP, piece, head)
            o_store(step, g).start()
            e = m * scale + jnp.log(l)
            for j in range(GROUP):
                logs = jnp.where(lane == g * GROUP + j, e[j * piece:(j + 1) * piece], logs)
            return logs

        now, before = scores(0), None
        for g in range(groups):
            later = scores(g + 1) if g + 1 < groups else None
            if before is not None:
                logs = finish(g - 1, logs, *before)
            before, now = weigh(*now), later
        logs = finish(groups - 1, logs, *before)
        lse_ref[:, pl.ds(seq, 1), :] = logs.T[:heads][:, None, :]

    n_ref[0] = jnp.where(me >= 2, 4, 2)
    if first:
        load(0)
    else:
        q_buf[0] = q_in[...]
        there = pl.ds(pl.multiple_of(jnp.where(odd == 1, 1, 3) * piece, piece), piece)
        for half, buf in enumerate((k_buf, v_buf)):
            buf[0, :piece] = kv_in[2 * half]
            buf[0, there] = kv_in[2 * half + 1]
        lse_ref[...] = lse_in[...]

    @pl.loop(0, size)
    def _(step):
        @pl.when((step > 0) | first)
        def _():
            for copy in kv_loads(step):
                copy.wait()
            for g in range(groups):
                q_load(step, g).wait()

        @pl.when((step == 0) & (size > 1))
        def _():
            load(1)

        @pl.when(step + 2 < size)
        def _():
            load(step + 2)

        if not last:
            @pl.when(step == max(size - 2, 0))
            def _():
                for copy in aheads():
                    copy.start()

        @pl.when(step >= 2)
        def _():
            for g in range(groups):
                o_store(step - 2, g).wait()

        place(step)
        need = n_ref[0]
        for count in (2, 3, 4):
            @pl.when((need == count) | (count == 2 and need == 1))
            def _():
                run(count, step, cut_ref[pl.ds(base + step, 1), :])

        @pl.when(step == 0)
        def _():
            scalars.wait()

        n_ref[0] = s_ref[jnp.minimum(base + step + 1, batch - 1)]

    if not last:
        for copy in aheads():
            copy.wait()
    for step in range(max(size - 2, 0), size):
        for g in range(groups):
            o_store(step, g).wait()


def attend(n, needs, cuts, q, k, v, near, fara, farb, prev):
    batch, heads, piece, head = q.shape
    base, size = BOUNDS[n], CHUNKS[n]
    first, last = prev is None, n == len(CHUNKS) - 1
    hbm = pl.BlockSpec(memory_space=pltpu.HBM)
    vmem = pl.BlockSpec(memory_space=pltpu.VMEM)
    in_specs = [hbm, vmem] + [hbm] * 4 + [vmem] * 2
    needs, q, k, v, near = (pltpu.with_memory_space_constraint(x, pltpu.HBM) for x in (needs, q, k, v, near))
    args = [needs, cuts, q, k, v, near, fara, farb]
    aliases = {}
    if not first:
        in_specs += [hbm, vmem, vmem, vmem]
        args += list(prev)
        aliases = {8: 0}
    out_shape = [
        jax.ShapeDtypeStruct(q.shape, jnp.bfloat16),
        jax.ShapeDtypeStruct((heads, batch, piece), jnp.float32),
    ]
    if not last:
        out_shape += [
            jax.ShapeDtypeStruct(q.shape[1:], jnp.bfloat16),
            jax.ShapeDtypeStruct((4, piece, head), jnp.bfloat16),
        ]
    return pl.pallas_call(
        functools.partial(attend_kernel, first, last, base, size),
        in_specs=in_specs,
        out_specs=[hbm] + [vmem] * (len(out_shape) - 1),
        scratch_shapes=[
            pltpu.SMEM(needs.shape, jnp.int32),
            pltpu.SMEM((1,), jnp.int32),
            pltpu.VMEM((DEPTH, heads, piece, head), jnp.bfloat16),
            pltpu.VMEM((DEPTH, 4 * piece, head), jnp.bfloat16),
            pltpu.VMEM((DEPTH, 4 * piece, head), jnp.bfloat16),
            pltpu.VMEM((2, heads, piece, head), jnp.bfloat16),
            pltpu.SemaphoreType.DMA,
            pltpu.SemaphoreType.DMA((DEPTH,)),
            pltpu.SemaphoreType.DMA((DEPTH, heads // GROUP)),
            pltpu.SemaphoreType.DMA((2, heads // GROUP)),
            pltpu.SemaphoreType.DMA,
        ],
        out_shape=out_shape,
        input_output_aliases=aliases,
        compiler_params=pltpu.CompilerParams(vmem_limit_bytes=32 << 20),
        cost_estimate=pl.CostEstimate(
            flops=size * heads * piece * 4 * piece * head * 4,
            bytes_accessed=size * heads * piece * head * 4,
            transcendentals=0,
        ),
    )(*args)


def shift(x, pairs):
    return lax.ppermute(x, "cp", pairs)


def solution(mesh):
    def local(q_loc, k_loc, v_loc, seg_loc):
        batch, piece, _, _ = q_loc.shape
        me = lax.axis_index("cp")
        q = jnp.transpose(q_loc, (0, 2, 1, 3))
        ranges = tuple(zip(BOUNDS[:-1], BOUNDS[1:]))
        sends = pack(ranges[:1], (True,), seg_loc, k_loc, v_loc)
        *more, whole = pack(ranges[1:] + ((0, batch),), (False,) * len(ranges[1:]) + (True,), seg_loc, k_loc, v_loc)
        sends = list(sends) + more
        fara = [shift(x, ACROSS) for x in sends]
        near = shift(whole, BESIDE)
        farb = [shift(x, SWAP) for x in fara]

        def zeros(packed, there):
            return jnp.where(there, packed[-batch:, 0].astype(jnp.int32), 0)

        odd, upper = me % 2 == 1, me >= 2
        cuts = zeros(whole, True) + zeros(near, odd) + zeros(fara[0], upper) + zeros(farb[0], upper)
        need = jnp.where(cuts <= me * piece, me - cuts // piece, me) + 1
        table = jnp.broadcast_to((cuts - me * piece)[:, None], (batch, piece))
        state = None
        for n in range(len(CHUNKS)):
            state = attend(n, need.astype(jnp.int32), table, q, k_loc, v_loc, near, fara[n], farb[n], state)
        out, lse = state[:2]
        return jnp.transpose(out, (0, 2, 1, 3)), jnp.transpose(lse, (1, 2, 0))

    return jax.shard_map(
        local,
        mesh=mesh,
        in_specs=(P("dp", "cp", None, None), P("dp", "cp", None), P("dp", "cp", None), P("dp", "cp")),
        out_specs=(P("dp", "cp", None, None), P("dp", "cp", None)),
        check_vma=False,
    )
```

profile of v0, /device:TPU:7, one launch (start us, length us, event | category | flops | bytes accessed | tf_op | source)
XLA Modules:
  0.0 160.9 jit_solution(8685116892429353500)
XLA Ops:
  0.6 5.7 %shard_map.59 = (bf16[1536,256]{1,0:T(8,128)(2,1)S(1)}, bf16[1280,256]{1,0:T(8,128)(2,1)S(1)}, bf16[1280,256]{1,0:T(8,128)(2,1)S(1)}, bf16[1280,256]{1,0:T(8,128...) custom-call(s32[32,128]{1,0:T(8,128)} %seg_ref.3, bf16[32,128,256]{2,1,0:T(8,128)(2,1)} %k_ref.15, ...), custom_call_target="tpu_custom_call" | custom-call | flops 1048576 | bytes 4194304 | tf_op jit(solution)/shard_map/pallas_call | solution.py:55
  6.4 1.3 collective-permute-start
  7.7 1.2 shard_map.60
  8.9 1.3 collective-permute-start.1
  10.2 1.3 collective-permute-start.9
  11.5 1.3 collective-permute-start.7
  12.8 1.3 collective-permute-start.11
  14.1 13.1 %collective-permute-done.1.fara_ref = bf16[1568,256]{1,0:T(8,128)(2,1)S(1)} collective-permute-done((bf16[1568,256]{1,0:T(8,128)(2,1)S(1)}, bf16[1568,256]{1,0:T(8,128)(2,1)S(1)}, u32[]{:S(2)}, u32[]{:S(2)}) %collective-permute-start.1) | collective-permute-done | bytes 802848 | tf_op jit(solution)/shard_map/ppermute | solution.py:283
  27.2 9.3 %collective-permute-start.2 = (bf16[1568,256]{1,0:T(8,128)(2,1)S(1)}, bf16[1568,256]{1,0:T(8,128)(2,1)S(1)}, u32[]{:S(2)}, u32[]{:S(2)}) collective-permute-start(bf16[1568,256]{1,0:T(8,128)(2,1)S(1)} %collective-permute-done.1.fara_ref), channel_id=1, source_target_pairs={{2,3},{3,2},{6,7},{7,6}} | collective-permute-start | bytes 2408456 | tf_op jit(solution)/shard_map/ppermute | solution.py:283
  36.5 4.7 %collective-permute-done.9.fara_ref = bf16[1280,256]{1,0:T(8,128)(2,1)S(1)} collective-permute-done((bf16[1280,256]{1,0:T(8,128)(2,1)S(1)}, bf16[1280,256]{1,0:T(8,128)(2,1)S(1)}, u32[]{:S(2)}, u32[]{:S(2)}) %collective-permute-start.9) | collective-permute-done | bytes 655392 | tf_op jit(solution)/shard_map/ppermute | solution.py:283
  41.2 0.0 copy-start.2
  41.2 1.3 collective-permute-start.5
  42.5 12.8 %collective-permute-done.7.fara_ref = bf16[1280,256]{1,0:T(8,128)(2,1)S(1)} collective-permute-done((bf16[1280,256]{1,0:T(8,128)(2,1)S(1)}, bf16[1280,256]{1,0:T(8,128)(2,1)S(1)}, u32[]{:S(2)}, u32[]{:S(2)}) %collective-permute-start.7) | collective-permute-done | bytes 655392 | tf_op jit(solution)/shard_map/ppermute | solution.py:283
  55.3 0.0 copy-start
  55.3 1.3 collective-permute-start.3
  56.5 15.6 %collective-permute-done.11.fara_ref = bf16[1536,256]{1,0:T(8,128)(2,1)S(1)} collective-permute-done((bf16[1536,256]{1,0:T(8,128)(2,1)S(1)}, bf16[1536,256]{1,0:T(8,128)(2,1)S(1)}, u32[]{:S(2)}, u32[]{:S(2)}) %collective-permute-start.11) | collective-permute-done | bytes 786464 | tf_op jit(solution)/shard_map/ppermute | solution.py:283
  72.1 0.0 copy-done
  72.1 9.3 %collective-permute-start.12 = (bf16[1536,256]{1,0:T(8,128)(2,1)S(1)}, bf16[1536,256]{1,0:T(8,128)(2,1)S(1)}, u32[]{:S(2)}, u32[]{:S(2)}) collective-permute-start(bf16[1536,256]{1,0:T(8,128)(2,1)S(1)} %collective-permute-done.11.fara_ref), channel_id=1, source_target_pairs={{2,3},{3,2},{6,7},{7,6}} | collective-permute-start | bytes 2359304 | tf_op jit(solution)/shard_map/ppermute | solution.py:283
  81.5 0.0 copy-done.2
  81.5 4.8 %collective-permute-done.5.fara_ref = bf16[1280,256]{1,0:T(8,128)(2,1)} collective-permute-done((bf16[1280,256]{1,0:T(8,128)(2,1)}, bf16[1280,256]{1,0:T(8,128)(2,1)}, u32[]{:S(2)}, u32[]{:S(2)}) %collective-permute-start.5) | collective-permute-done | bytes 655392 | tf_op jit(solution)/shard_map/ppermute | solution.py:283
  86.3 9.3 %collective-permute-start.10 = (bf16[1280,256]{1,0:T(8,128)(2,1)}, bf16[1280,256]{1,0:T(8,128)(2,1)S(1)}, u32[]{:S(2)}, u32[]{:S(2)}) collective-permute-start(bf16[1280,256]{1,0:T(8,128)(2,1)} %copy-done.2), channel_id=1, source_target_pairs={{2,3},{3,2},{6,7},{7,6}} | collective-permute-start | bytes 1966088 | tf_op jit(solution)/shard_map/ppermute | solution.py:283
  95.6 4.7 %collective-permute-done.3.fara_ref = bf16[1280,256]{1,0:T(8,128)(2,1)} collective-permute-done((bf16[1280,256]{1,0:T(8,128)(2,1)}, bf16[1280,256]{1,0:T(8,128)(2,1)}, u32[]{:S(2)}, u32[]{:S(2)}) %collective-permute-start.3) | collective-permute-done | bytes 655392 | tf_op jit(solution)/shard_map/ppermute | solution.py:283
  100.3 5.8 %collective-permute-start.8 = (bf16[1280,256]{1,0:T(8,128)(2,1)}, bf16[1280,256]{1,0:T(8,128)(2,1)S(1)}, u32[]{:S(2)}, u32[]{:S(2)}) collective-permute-start(bf16[1280,256]{1,0:T(8,128)(2,1)} %copy-done), channel_id=1, source_target_pairs={{2,3},{3,2},{6,7},{7,6}} | collective-permute-start | bytes 1966088 | tf_op jit(solution)/shard_map/ppermute | solution.py:283
  106.1 0.0 collective-permute-done.2.farb_ref
  106.1 1.9 %collective-permute-start.6 = (bf16[1280,256]{1,0:T(8,128)(2,1)}, bf16[1280,256]{1,0:T(8,128)(2,1)S(1)}, u32[]{:S(2)}, u32[]{:S(2)}) collective-permute-start(bf16[1280,256]{1,0:T(8,128)(2,1)} %collective-permute-done.5.fara_ref), channel_id=1, source_target_pairs={{2,3},{3,2},{6,7},{7,6}} | collective-permute-start | bytes 1966088 | tf_op jit(solution)/shard_map/ppermute | solution.py:283
  108.1 0.0 collective-permute-done.near_ref
  108.1 2.4 %collective-permute-start.4 = (bf16[1280,256]{1,0:T(8,128)(2,1)}, bf16[1280,256]{1,0:T(8,128)(2,1)S(1)}, u32[]{:S(2)}, u32[]{:S(2)}) collective-permute-start(bf16[1280,256]{1,0:T(8,128)(2,1)} %collective-permute-done.3.fara_ref), channel_id=1, source_target_pairs={{2,3},{3,2},{6,7},{7,6}} | collective-permute-start | bytes 1966088 | tf_op jit(solution)/shard_map/ppermute | solution.py:283
  110.5 0.8 subtract_reduce_fusion
  111.3 0.6 fusion.s_hbm
  111.9 0.1 broadcast_in_dim.23.cut_ref
  112.0 9.7 %shard_map.61 = (bf16[32,10,128,256]{3,2,1,0:T(8,128)(2,1)}, f32[10,32,128]{2,1,0:T(8,128)S(1)}, bf16[10,128,256]{2,1,0:T(8,128)(2,1)S(1)}, bf16[4,128,256]{2,1,0:T(8,128)(2,1)S(1)}) custom-call(s32[32]{0:T(128)} %fusion.s_hbm, s32[32,128]{1,0:T(8,128)S(1)} %broadcast_in_dim.23.cut_ref, bf16[32,10,128,256]{3,2,1,0:T(8,128)(2,1)} %bitcast.3, ...), custom_call_target="tpu_custom_call" | custom-call | flops 4026531840 | bytes 7864320 | tf_op jit(solution)/shard_map/pallas_call | solution.py:254
  121.7 0.0 collective-permute-done.12.farb_ref
  121.7 0.0 copy-start.3
  121.7 8.9 %shard_map.62 = (bf16[32,10,128,256]{3,2,1,0:T(8,128)(2,1)}, f32[10,32,128]{2,1,0:T(8,128)S(1)}, bf16[10,128,256]{2,1,0:T(8,128)(2,1)S(1)}, bf16[4,128,256]{2,1,0:T(8,128)(2,1)S(1)}) custom-call(s32[32]{0:T(128)} %fusion.s_hbm, s32[32,128]{1,0:T(8,128)S(1)} %broadcast_in_dim.23.cut_ref, ...), custom_call_target="tpu_custom_call", output_to_operand_aliasing={{0}: (8, {})} | custom-call | flops 4026531840 | bytes 7864320 | tf_op jit(solution)/shard_map/pallas_call | solution.py:254
  130.6 0.0 collective-permute-done.10.farb_ref
  130.6 0.0 copy-done.3
  130.7 0.0 copy-start.1
  130.7 6.6 %shard_map.63 = (bf16[32,10,128,256]{3,2,1,0:T(8,128)(2,1)}, f32[10,32,128]{2,1,0:T(8,128)S(1)}, bf16[10,128,256]{2,1,0:T(8,128)(2,1)S(1)}, bf16[4,128,256]{2,1,0:T(8,128)(2,1)S(1)}) custom-call(s32[32]{0:T(128)} %fusion.s_hbm, s32[32,128]{1,0:T(8,128)S(1)} %broadcast_in_dim.23.cut_ref, ...), custom_call_target="tpu_custom_call", output_to_operand_aliasing={{0}: (8, {})} | custom-call | flops 3355443200 | bytes 6553600 | tf_op jit(solution)/shard_map/pallas_call | solution.py:254
  137.3 0.0 collective-permute-done.8.farb_ref
  137.3 0.0 copy-done.1
  137.3 7.2 %shard_map.64 = (bf16[32,10,128,256]{3,2,1,0:T(8,128)(2,1)}, f32[10,32,128]{2,1,0:T(8,128)S(1)}, bf16[10,128,256]{2,1,0:T(8,128)(2,1)S(1)}, bf16[4,128,256]{2,1,0:T(8,128)(2,1)S(1)}) custom-call(s32[32]{0:T(128)} %fusion.s_hbm, s32[32,128]{1,0:T(8,128)S(1)} %broadcast_in_dim.23.cut_ref, ...), custom_call_target="tpu_custom_call", output_to_operand_aliasing={{0}: (8, {})} | custom-call | flops 3355443200 | bytes 6553600 | tf_op jit(solution)/shard_map/pallas_call | solution.py:254
  144.6 0.0 collective-permute-done.6.farb_ref
  144.6 8.1 %shard_map.65 = (bf16[32,10,128,256]{3,2,1,0:T(8,128)(2,1)}, f32[10,32,128]{2,1,0:T(8,128)S(1)}, bf16[10,128,256]{2,1,0:T(8,128)(2,1)S(1)}, bf16[4,128,256]{2,1,0:T(8,128)(2,1)S(1)}) custom-call(s32[32]{0:T(128)} %fusion.s_hbm, s32[32,128]{1,0:T(8,128)S(1)} %broadcast_in_dim.23.cut_ref, ...), custom_call_target="tpu_custom_call", output_to_operand_aliasing={{0}: (8, {})} | custom-call | flops 3355443200 | bytes 6553600 | tf_op jit(solution)/shard_map/pallas_call | solution.py:254
  152.7 0.0 collective-permute-done.4.farb_ref
  152.7 8.0 %shard_map.66 = (bf16[32,10,128,256]{3,2,1,0:T(8,128)(2,1)}, f32[10,32,128]{2,1,0:T(8,128)}) custom-call(s32[32]{0:T(128)} %fusion.s_hbm, s32[32,128]{1,0:T(8,128)S(1)} %broadcast_in_dim.23.cut_ref, bf16[32,10,128,256]{3,2,1,0:T(8,128)(2,1)} %bitcast.8, bf16[32,128,256]{2,1,0:T(8,128)(2,1)} %k_ref.15, ...), custom_call_target="tpu_custom_call", output_to_operand_aliasing={{0}: (8, {})} | custom-call | flops 3355443200 | bytes 6553600 | tf_op jit(solution)/shard_map/pallas_call | solution.py:254
Async XLA Ops:
  6.4 101.7 %collective-permute-start = (bf16[8224,256]{1,0:T(8,128)(2,1)}, bf16[8224,256]{1,0:T(8,128)(2,1)}, u32[]{:S(2)}, u32[]{:S(2)}) collective-permute-start(bf16[8224,256]{1,0:T(8,128)(2,1)} %get-tuple-element.30), channel_id=1, source_target_pairs={{0,1},{2,3},{4,5},{6,7}} | collective-permute-start | bytes 12632072 | tf_op jit(solution)/shard_map/ppermute | solution.py:283
  8.9 18.3 %collective-permute-start.1 = (bf16[1568,256]{1,0:T(8,128)(2,1)S(1)}, bf16[1568,256]{1,0:T(8,128)(2,1)S(1)}, u32[]{:S(2)}, u32[]{:S(2)}) collective-permute-start(bf16[1568,256]{1,0:T(8,128)(2,1)S(1)} %shard_map.60), channel_id=1, source_target_pairs={{0,2},{1,3},{4,6},{5,7}} | collective-permute-start | bytes 2408456 | tf_op jit(solution)/shard_map/ppermute | solution.py:283
  10.2 31.0 %collective-permute-start.9 = (bf16[1280,256]{1,0:T(8,128)(2,1)S(1)}, bf16[1280,256]{1,0:T(8,128)(2,1)S(1)}, u32[]{:S(2)}, u32[]{:S(2)}) collective-permute-start(bf16[1280,256]{1,0:T(8,128)(2,1)S(1)} %get-tuple-element.34), channel_id=1, source_target_pairs={{0,2},{1,3},{4,6},{5,7}} | collective-permute-start | bytes 1966088 | tf_op jit(solution)/shard_map/ppermute | solution.py:283
  11.5 43.8 %collective-permute-start.7 = (bf16[1280,256]{1,0:T(8,128)(2,1)S(1)}, bf16[1280,256]{1,0:T(8,128)(2,1)S(1)}, u32[]{:S(2)}, u32[]{:S(2)}) collective-permute-start(bf16[1280,256]{1,0:T(8,128)(2,1)S(1)} %get-tuple-element.33), channel_id=1, source_target_pairs={{0,2},{1,3},{4,6},{5,7}} | collective-permute-start | bytes 1966088 | tf_op jit(solution)/shard_map/ppermute | solution.py:283
  12.8 59.3 %collective-permute-start.11 = (bf16[1536,256]{1,0:T(8,128)(2,1)S(1)}, bf16[1536,256]{1,0:T(8,128)(2,1)S(1)}, u32[]{:S(2)}, u32[]{:S(2)}) collective-permute-start(bf16[1536,256]{1,0:T(8,128)(2,1)S(1)} %get-tuple-element.35), channel_id=1, source_target_pairs={{0,2},{1,3},{4,6},{5,7}} | collective-permute-start | bytes 2359304 | tf_op jit(solution)/shard_map/ppermute | solution.py:283
  27.2 79.0 %collective-permute-start.2 = (bf16[1568,256]{1,0:T(8,128)(2,1)S(1)}, bf16[1568,256]{1,0:T(8,128)(2,1)S(1)}, u32[]{:S(2)}, u32[]{:S(2)}) collective-permute-start(bf16[1568,256]{1,0:T(8,128)(2,1)S(1)} %collective-permute-done.1.fara_ref), channel_id=1, source_target_pairs={{2,3},{3,2},{6,7},{7,6}} | collective-permute-start | bytes 2408456 | tf_op jit(solution)/shard_map/ppermute | solution.py:283
  41.2 40.3 %copy-start.2 = (bf16[1280,256]{1,0:T(8,128)(2,1)}, bf16[1280,256]{1,0:T(8,128)(2,1)S(1)}, u32[]{:S(2)}) copy-start(bf16[1280,256]{1,0:T(8,128)(2,1)S(1)} %collective-permute-done.9.fara_ref) | copy-start | bytes 1966084
  41.2 45.0 %collective-permute-start.5 = (bf16[1280,256]{1,0:T(8,128)(2,1)}, bf16[1280,256]{1,0:T(8,128)(2,1)}, u32[]{:S(2)}, u32[]{:S(2)}) collective-permute-start(bf16[1280,256]{1,0:T(8,128)(2,1)} %get-tuple-element.32), channel_id=1, source_target_pairs={{0,2},{1,3},{4,6},{5,7}} | collective-permute-start | bytes 1966088 | tf_op jit(solution)/shard_map/ppermute | solution.py:283
  55.3 16.9 %copy-start = (bf16[1280,256]{1,0:T(8,128)(2,1)}, bf16[1280,256]{1,0:T(8,128)(2,1)S(1)}, u32[]{:S(2)}) copy-start(bf16[1280,256]{1,0:T(8,128)(2,1)S(1)} %collective-permute-done.7.fara_ref) | copy-start | bytes 1966084
  55.3 45.0 %collective-permute-start.3 = (bf16[1280,256]{1,0:T(8,128)(2,1)}, bf16[1280,256]{1,0:T(8,128)(2,1)}, u32[]{:S(2)}, u32[]{:S(2)}) collective-permute-start(bf16[1280,256]{1,0:T(8,128)(2,1)} %get-tuple-element.31), channel_id=1, source_target_pairs={{0,2},{1,3},{4,6},{5,7}} | collective-permute-start | bytes 1966088 | tf_op jit(solution)/shard_map/ppermute | solution.py:283
  72.1 49.6 %collective-permute-start.12 = (bf16[1536,256]{1,0:T(8,128)(2,1)S(1)}, bf16[1536,256]{1,0:T(8,128)(2,1)S(1)}, u32[]{:S(2)}, u32[]{:S(2)}) collective-permute-start(bf16[1536,256]{1,0:T(8,128)(2,1)S(1)} %collective-permute-done.11.fara_ref), channel_id=1, source_target_pairs={{2,3},{3,2},{6,7},{7,6}} | collective-permute-start | bytes 2359304 | tf_op jit(solution)/shard_map/ppermute | solution.py:283
  86.3 44.4 %collective-permute-start.10 = (bf16[1280,256]{1,0:T(8,128)(2,1)}, bf16[1280,256]{1,0:T(8,128)(2,1)S(1)}, u32[]{:S(2)}, u32[]{:S(2)}) collective-permute-start(bf16[1280,256]{1,0:T(8,128)(2,1)} %copy-done.2), channel_id=1, source_target_pairs={{2,3},{3,2},{6,7},{7,6}} | collective-permute-start | bytes 1966088 | tf_op jit(solution)/shard_map/ppermute | solution.py:283
  100.3 37.0 %collective-permute-start.8 = (bf16[1280,256]{1,0:T(8,128)(2,1)}, bf16[1280,256]{1,0:T(8,128)(2,1)S(1)}, u32[]{:S(2)}, u32[]{:S(2)}) collective-permute-start(bf16[1280,256]{1,0:T(8,128)(2,1)} %copy-done), channel_id=1, source_target_pairs={{2,3},{3,2},{6,7},{7,6}} | collective-permute-start | bytes 1966088 | tf_op jit(solution)/shard_map/ppermute | solution.py:283
  106.1 38.4 %collective-permute-start.6 = (bf16[1280,256]{1,0:T(8,128)(2,1)}, bf16[1280,256]{1,0:T(8,128)(2,1)S(1)}, u32[]{:S(2)}, u32[]{:S(2)}) collective-permute-start(bf16[1280,256]{1,0:T(8,128)(2,1)} %collective-permute-done.5.fara_ref), channel_id=1, source_target_pairs={{2,3},{3,2},{6,7},{7,6}} | collective-permute-start | bytes 1966088 | tf_op jit(solution)/shard_map/ppermute | solution.py:283
  108.1 44.7 %collective-permute-start.4 = (bf16[1280,256]{1,0:T(8,128)(2,1)}, bf16[1280,256]{1,0:T(8,128)(2,1)S(1)}, u32[]{:S(2)}, u32[]{:S(2)}) collective-permute-start(bf16[1280,256]{1,0:T(8,128)(2,1)} %collective-permute-done.3.fara_ref), channel_id=1, source_target_pairs={{2,3},{3,2},{6,7},{7,6}} | collective-permute-start | bytes 1966088 | tf_op jit(solution)/shard_map/ppermute | solution.py:283
  121.7 8.9 %copy-start.3 = (bf16[1280,256]{1,0:T(8,128)(2,1)S(1)}, bf16[1280,256]{1,0:T(8,128)(2,1)}, u32[]{:S(2)}) copy-start(bf16[1280,256]{1,0:T(8,128)(2,1)} %copy-done.2) | copy-start | bytes 1966084
  130.7 6.6 %copy-start.1 = (bf16[1280,256]{1,0:T(8,128)(2,1)S(1)}, bf16[1280,256]{1,0:T(8,128)(2,1)}, u32[]{:S(2)}) copy-start(bf16[1280,256]{1,0:T(8,128)(2,1)} %copy-done) | copy-start | bytes 1966084
where the time goes:
time: 162 us; the launch traced here: 161 us
  Pallas kernels  55.6 us (34%)
  waiting for transfers between devices  55.6 us (34%)
  starting transfers between devices  47.2 us (29%)
    ppermute x13, waiting for transfers between devices, shift(): return lax.ppermute(x, 'cp', pairs)  55.6 us
    pallas_call x6, Pallas kernels, attend(): pl.pallas_call(functools.partial(attend_kernel, first, last, base, size),...  48.7 us
    ppermute x13, starting transfers between devices, shift(): return lax.ppermute(x, 'cp', pairs)  47.2 us
    pallas_call x2, Pallas kernels, pack(): pl.pallas_call(functools.partial(pack_kernel, ranges, tails), in_specs=[h...  6.94 us
  transfers between devices with their start and end apart: 13, of which 6 were waited for; matrix products, arithmetic and copies ran while one was open for 1% of the time, Pallas kernels for 26%

commit v1 on v0

--- a/solution.py
+++ b/solution.py
@@ -8,7 +8,7 @@
 from jax.sharding import PartitionSpec as P
 
 
-CHUNKS = (6, 6, 5, 5, 5, 5)
+CHUNKS = (6, 6, 6, 6, 5, 3)
 BOUNDS = tuple(sum(CHUNKS[:n]) for n in range(len(CHUNKS) + 1))
 GROUP = 2
 DEPTH = 3
@@ -16,7 +16,6 @@
 
 ACROSS = [(0, 2), (1, 3)]
 BESIDE = [(0, 1), (2, 3)]
-SWAP = [(2, 3), (3, 2)]
 
 
 def pack_kernel(ranges, tails, seg_ref, k_ref, v_ref, *rest):
@@ -279,6 +278,39 @@
     )(*args)
 
 
+def swap_kernel(mine_ref, other_ref, send_sem, recv_sem):
+    me = lax.axis_index("cp")
+    partner = {"cp": me + 1 - 2 * lax.rem(me, 2)}
+    barrier = pltpu.get_barrier_semaphore()
+    pl.semaphore_signal(barrier, inc=1, device_id=partner, device_id_type=pl.DeviceIdType.MESH)
+    pl.semaphore_wait(barrier, 1)
+    copy = pltpu.make_async_remote_copy(
+        src_ref=mine_ref,
+        dst_ref=other_ref,
+        send_sem=send_sem,
+        recv_sem=recv_sem,
+        device_id=partner,
+        device_id_type=pl.DeviceIdType.MESH,
+    )
+    copy.start()
+    copy.wait()
+
+
+def swap(n, x):
+    vmem = pl.BlockSpec(memory_space=pltpu.VMEM)
+    return pl.pallas_call(
+        swap_kernel,
+        in_specs=[vmem],
+        out_specs=vmem,
+        out_shape=jax.ShapeDtypeStruct(x.shape, x.dtype),
+        scratch_shapes=[pltpu.SemaphoreType.DMA, pltpu.SemaphoreType.DMA],
+        compiler_params=pltpu.CompilerParams(
+            collective_id=n, has_side_effects=True, vmem_limit_bytes=16 << 20
+        ),
+        cost_estimate=pl.CostEstimate(flops=1 << 20, bytes_accessed=4 * x.size, transcendentals=0),
+    )(x)
+
+
 def shift(x, pairs):
     return lax.ppermute(x, "cp", pairs)
 
@@ -294,7 +326,7 @@
         sends = list(sends) + more
         fara = [shift(x, ACROSS) for x in sends]
         near = shift(whole, BESIDE)
-        farb = [shift(x, SWAP) for x in fara]
+        farb = [swap(n, x) for n, x in enumerate(fara)]
 
         def zeros(packed, there):
             return jnp.where(there, packed[-batch:, 0].astype(jnp.int32), 0)

time: 162 us -> 157 us (0.969)
  starting transfers between devices: 47.2 us -> 9.02 us
  Pallas kernels: 55.6 us -> 92.3 us
  waiting for transfers between devices: 55.6 us -> 49.7 us
  local copies, waits for them, and re-layouts: 0.09 us -> 1.99 us
    ppermute x13 -> x7, starting transfers between devices: 47.2 us -> 9.02 us  [shift(): return lax.ppermute(x, 'cp', pairs)]
    pallas_call x0 -> x6, Pallas kernels: none -> 37.9 us  [swap(): pl.pallas_call(swap_kernel, in_specs=[vmem], out_specs=vmem, out_shape=ja...]
    ppermute x13 -> x7, waiting for transfers between devices: 55.6 us -> 49.7 us  [shift(): return lax.ppermute(x, 'cp', pairs)]
    pallas_call x6, Pallas kernels: 48.7 us -> 46.2 us  [attend(): pl.pallas_call(functools.partial(attend_kernel, first, last, base, size),...]
    unnamed x8 -> x6, local copies, waits for them, and re-layouts: 0.02 us -> 1.92 us
  transfers between devices with their start and end apart: 13 -> 7, of which waited for: 6 -> 4; matrix products, arithmetic and copies ran while one was open for 1% -> 0% of each run, Pallas kernels for 26% -> 26%
where the time goes in v1:
time: 157 us; the launch traced here: 155 us
  Pallas kernels  92.3 us (59%)
  waiting for transfers between devices  49.7 us (32%)
  starting transfers between devices  9.02 us (6%)
  local copies, waits for them, and re-layouts  1.99 us (1%)
    ppermute x7, waiting for transfers between devices, shift(): return lax.ppermute(x, 'cp', pairs)  49.7 us
    pallas_call x6, Pallas kernels, attend(): pl.pallas_call(functools.partial(attend_kernel, first, last, base, size),...  46.2 us
    pallas_call x6, Pallas kernels, swap(): pl.pallas_call(swap_kernel, in_specs=[vmem], out_specs=vmem, out_shape=ja...  37.9 us
    ppermute x7, starting transfers between devices, shift(): return lax.ppermute(x, 'cp', pairs)  9.02 us
    pallas_call x2, Pallas kernels, pack(): pl.pallas_call(functools.partial(pack_kernel, ranges, tails), in_specs=[h...  8.19 us
  transfers between devices with their start and end apart: 7, of which 4 were waited for; matrix products, arithmetic and copies ran while one was open for 0% of the time, Pallas kernels for 26%

profile of v1, /device:TPU:7, one launch (start us, length us, event | category | flops | bytes accessed | tf_op | source)
XLA Modules:
  0.0 155.5 jit_solution(17681304045619195094)
XLA Ops:
  0.6 6.1 %shard_map.59 = (bf16[1536,256]{1,0:T(8,128)(2,1)}, bf16[1536,256]{1,0:T(8,128)(2,1)}, bf16[1536,256]{1,0:T(8,128)(2,1)}, bf16[1280,256]{1,0:T(8,128)(2,1)S(1)},...) custom-call(s32[32,128]{1,0:T(8,128)} %seg_ref.3, bf16[32,128,256]{2,1,0:T(8,128)(2,1)} %k_ref.15, ...), custom_call_target="tpu_custom_call" | custom-call | flops 1048576 | bytes 4194304 | tf_op jit(solution)/shard_map/pallas_call | solution.py:54
  6.7 1.3 collective-permute-start
  8.0 1.3 collective-permute-start.3
  9.3 1.3 collective-permute-start.2
  10.6 2.1 %shard_map.60 = bf16[1568,256]{1,0:T(8,128)(2,1)} custom-call(s32[32,128]{1,0:T(8,128)} %seg_ref.3, bf16[32,128,256]{2,1,0:T(8,128)(2,1)} %k_ref.15, bf16[32,128,256]{2,1,0:T(8,128)(2,1)} %v_ref.15), custom_call_target="tpu_custom_call" | custom-call | flops 1048576 | bytes 4194304 | tf_op jit(solution)/shard_map/pallas_call | solution.py:54
  12.7 1.3 collective-permute-start.1
  14.0 1.3 collective-permute-start.6
  15.3 16.2 %collective-permute-done.2.mine_ref.fara_ref = bf16[768,256]{1,0:T(8,128)(2,1)S(1)} collective-permute-done((bf16[768,256]{1,0:T(8,128)(2,1)S(1)}, bf16[768,256]{1,0:T(8,128)(2,1)S(1)}, u32[]{:S(2)}, u32[]{:S(2)}) %collective-permute-start.2) | collective-permute-done | bytes 393248 | tf_op jit(solution)/shard_map/ppermute | solution.py:315
  31.6 1.3 collective-permute-start.5
  32.9 0.0 collective-permute-done.3.mine_ref.fara_ref
  32.9 0.0 copy-start
  32.9 0.8 copy-done
  33.7 1.3 collective-permute-start.4
  35.0 8.8 %shard_map.62.farb_ref = bf16[768,256]{1,0:T(8,128)(2,1)S(1)} custom-call(bf16[768,256]{1,0:T(8,128)(2,1)S(1)} %collective-permute-done.2.mine_ref.fara_ref), custom_call_target="tpu_custom_call" | custom-call | flops 1048576 | bytes 786432 | tf_op jit(solution)/shard_map/pallas_call | solution.py:301
  43.9 0.0 copy-start.1
  43.9 1.1 copy-done.1
  44.9 2.1 %shard_map.63.farb_ref = bf16[1280,256]{1,0:T(8,128)(2,1)S(1)} custom-call(bf16[1280,256]{1,0:T(8,128)(2,1)S(1)} %copy-done.1), custom_call_target="tpu_custom_call" | custom-call | flops 1048576 | bytes 1310720 | tf_op jit(solution)/shard_map/pallas_call | solution.py:301
  47.1 18.6 %collective-permute-done.6.mine_ref.fara_ref = bf16[1536,256]{1,0:T(8,128)(2,1)S(1)} collective-permute-done((bf16[1536,256]{1,0:T(8,128)(2,1)}, bf16[1536,256]{1,0:T(8,128)(2,1)S(1)}, u32[]{:S(2)}, u32[]{:S(2)}) %collective-permute-start.6) | collective-permute-done | bytes 786464 | tf_op jit(solution)/shard_map/ppermute | solution.py:315
  65.6 9.4 %shard_map.66.farb_ref = bf16[1536,256]{1,0:T(8,128)(2,1)S(1)} custom-call(bf16[1536,256]{1,0:T(8,128)(2,1)S(1)} %collective-permute-done.6.mine_ref.fara_ref), custom_call_target="tpu_custom_call" | custom-call | flops 1048576 | bytes 1572864 | tf_op jit(solution)/shard_map/pallas_call | solution.py:301
  75.0 7.5 %collective-permute-done.5.mine_ref.fara_ref = bf16[1536,256]{1,0:T(8,128)(2,1)S(1)} collective-permute-done((bf16[1536,256]{1,0:T(8,128)(2,1)}, bf16[1536,256]{1,0:T(8,128)(2,1)S(1)}, u32[]{:S(2)}, u32[]{:S(2)}) %collective-permute-start.5) | collective-permute-done | bytes 786464 | tf_op jit(solution)/shard_map/ppermute | solution.py:315
  82.5 9.4 %shard_map.65.farb_ref = bf16[1536,256]{1,0:T(8,128)(2,1)S(1)} custom-call(bf16[1536,256]{1,0:T(8,128)(2,1)S(1)} %collective-permute-done.5.mine_ref.fara_ref), custom_call_target="tpu_custom_call" | custom-call | flops 1048576 | bytes 1572864 | tf_op jit(solution)/shard_map/pallas_call | solution.py:301
  91.9 7.5 %collective-permute-done.4.mine_ref.fara_ref = bf16[1536,256]{1,0:T(8,128)(2,1)S(1)} collective-permute-done((bf16[1536,256]{1,0:T(8,128)(2,1)}, bf16[1536,256]{1,0:T(8,128)(2,1)S(1)}, u32[]{:S(2)}, u32[]{:S(2)}) %collective-permute-start.4) | collective-permute-done | bytes 786464 | tf_op jit(solution)/shard_map/ppermute | solution.py:315
  99.3 5.9 %shard_map.64.farb_ref = bf16[1536,256]{1,0:T(8,128)(2,1)S(1)} custom-call(bf16[1536,256]{1,0:T(8,128)(2,1)S(1)} %collective-permute-done.4.mine_ref.fara_ref), custom_call_target="tpu_custom_call" | custom-call | flops 1048576 | bytes 1572864 | tf_op jit(solution)/shard_map/pallas_call | solution.py:301
  105.2 0.0 collective-permute-done.1.mine_ref.fara_ref
  105.2 2.3 %shard_map.61.farb_ref = bf16[1568,256]{1,0:T(8,128)(2,1)S(1)} custom-call(bf16[1568,256]{1,0:T(8,128)(2,1)S(1)} %collective-permute-done.1.mine_ref.fara_ref), custom_call_target="tpu_custom_call" | custom-call | flops 1048576 | bytes 1605632 | tf_op jit(solution)/shard_map/pallas_call | solution.py:301
  107.6 0.0 collective-permute-done.near_ref
  107.6 0.8 subtract_reduce_fusion
  108.4 0.6 fusion.s_hbm
  109.0 0.1 broadcast_in_dim.23.cut_ref
  109.1 9.7 %shard_map.67 = (bf16[32,10,128,256]{3,2,1,0:T(8,128)(2,1)}, f32[10,32,128]{2,1,0:T(8,128)S(1)}, bf16[10,128,256]{2,1,0:T(8,128)(2,1)S(1)}, bf16[4,128,256]{2,1,0:T(8,128)(2,1)S(1)}) custom-call(s32[32]{0:T(128)} %fusion.s_hbm, s32[32,128]{1,0:T(8,128)S(1)} %broadcast_in_dim.23.cut_ref, bf16[32,10,128,256]{3,2,1,0:T(8,128)(2,1)} %bitcast.3, ...), custom_call_target="tpu_custom_call" | custom-call | flops 4026531840 | bytes 7864320 | tf_op jit(solution)/shard_map/pallas_call | solution.py:253
  118.8 8.9 %shard_map.68 = (bf16[32,10,128,256]{3,2,1,0:T(8,128)(2,1)}, f32[10,32,128]{2,1,0:T(8,128)S(1)}, bf16[10,128,256]{2,1,0:T(8,128)(2,1)S(1)}, bf16[4,128,256]{2,1,0:T(8,128)(2,1)S(1)}) custom-call(s32[32]{0:T(128)} %fusion.s_hbm, s32[32,128]{1,0:T(8,128)S(1)} %broadcast_in_dim.23.cut_ref, ...), custom_call_target="tpu_custom_call", output_to_operand_aliasing={{0}: (8, {})} | custom-call | flops 4026531840 | bytes 7864320 | tf_op jit(solution)/shard_map/pallas_call | solution.py:253
  127.7 7.8 %shard_map.69 = (bf16[32,10,128,256]{3,2,1,0:T(8,128)(2,1)}, f32[10,32,128]{2,1,0:T(8,128)S(1)}, bf16[10,128,256]{2,1,0:T(8,128)(2,1)S(1)}, bf16[4,128,256]{2,1,0:T(8,128)(2,1)S(1)}) custom-call(s32[32]{0:T(128)} %fusion.s_hbm, s32[32,128]{1,0:T(8,128)S(1)} %broadcast_in_dim.23.cut_ref, ...), custom_call_target="tpu_custom_call", output_to_operand_aliasing={{0}: (8, {})} | custom-call | flops 4026531840 | bytes 7864320 | tf_op jit(solution)/shard_map/pallas_call | solution.py:253
  135.6 0.0 copy-start.2
  135.6 8.3 %shard_map.70 = (bf16[32,10,128,256]{3,2,1,0:T(8,128)(2,1)}, f32[10,32,128]{2,1,0:T(8,128)S(1)}, bf16[10,128,256]{2,1,0:T(8,128)(2,1)S(1)}, bf16[4,128,256]{2,1,0:T(8,128)(2,1)S(1)}) custom-call(s32[32]{0:T(128)} %fusion.s_hbm, s32[32,128]{1,0:T(8,128)S(1)} %broadcast_in_dim.23.cut_ref, ...), custom_call_target="tpu_custom_call", output_to_operand_aliasing={{0}: (8, {})} | custom-call | flops 4026531840 | bytes 7864320 | tf_op jit(solution)/shard_map/pallas_call | solution.py:253
  143.9 0.0 copy-done.2
  143.9 6.6 %shard_map.71 = (bf16[32,10,128,256]{3,2,1,0:T(8,128)(2,1)}, f32[10,32,128]{2,1,0:T(8,128)S(1)}, bf16[10,128,256]{2,1,0:T(8,128)(2,1)S(1)}, bf16[4,128,256]{2,1,0:T(8,128)(2,1)S(1)}) custom-call(s32[32]{0:T(128)} %fusion.s_hbm, s32[32,128]{1,0:T(8,128)S(1)} %broadcast_in_dim.23.cut_ref, ...), custom_call_target="tpu_custom_call", output_to_operand_aliasing={{0}: (8, {})} | custom-call | flops 3355443200 | bytes 6553600 | tf_op jit(solution)/shard_map/pallas_call | solution.py:253
  150.5 4.8 %shard_map.72 = (bf16[32,10,128,256]{3,2,1,0:T(8,128)(2,1)}, f32[10,32,128]{2,1,0:T(8,128)}) custom-call(s32[32]{0:T(128)} %fusion.s_hbm, s32[32,128]{1,0:T(8,128)S(1)} %broadcast_in_dim.23.cut_ref, bf16[32,10,128,256]{3,2,1,0:T(8,128)(2,1)} %bitcast.8, bf16[32,128,256]{2,1,0:T(8,128)(2,1)} %k_ref.15, ...), custom_call_target="tpu_custom_call", output_to_operand_aliasing={{0}: (8, {})} | custom-call | flops 2013265920 | bytes 3932160 | tf_op jit(solution)/shard_map/pallas_call | solution.py:253
Async XLA Ops:
  6.7 100.8 %collective-permute-start = (bf16[8224,256]{1,0:T(8,128)(2,1)}, bf16[8224,256]{1,0:T(8,128)(2,1)}, u32[]{:S(2)}, u32[]{:S(2)}) collective-permute-start(bf16[8224,256]{1,0:T(8,128)(2,1)} %get-tuple-element.30), channel_id=1, source_target_pairs={{0,1},{2,3},{4,5},{6,7}} | collective-permute-start | bytes 12632072 | tf_op jit(solution)/shard_map/ppermute | solution.py:315
  8.0 24.8 %collective-permute-start.3 = (bf16[1280,256]{1,0:T(8,128)(2,1)S(1)}, bf16[1280,256]{1,0:T(8,128)(2,1)S(1)}, u32[]{:S(2)}, u32[]{:S(2)}) collective-permute-start(bf16[1280,256]{1,0:T(8,128)(2,1)S(1)} %get-tuple-element.32), channel_id=1, source_target_pairs={{0,2},{1,3},{4,6},{5,7}} | collective-permute-start | bytes 1966088 | tf_op jit(solution)/shard_map/ppermute | solution.py:315
  9.3 22.2 %collective-permute-start.2 = (bf16[768,256]{1,0:T(8,128)(2,1)S(1)}, bf16[768,256]{1,0:T(8,128)(2,1)S(1)}, u32[]{:S(2)}, u32[]{:S(2)}) collective-permute-start(bf16[768,256]{1,0:T(8,128)(2,1)S(1)} %get-tuple-element.31), channel_id=1, source_target_pairs={{0,2},{1,3},{4,6},{5,7}} | collective-permute-start | bytes 1179656 | tf_op jit(solution)/shard_map/ppermute | solution.py:315
  12.7 92.5 %collective-permute-start.1 = (bf16[1568,256]{1,0:T(8,128)(2,1)}, bf16[1568,256]{1,0:T(8,128)(2,1)S(1)}, u32[]{:S(2)}, u32[]{:S(2)}) collective-permute-start(bf16[1568,256]{1,0:T(8,128)(2,1)} %shard_map.60), channel_id=1, source_target_pairs={{0,2},{1,3},{4,6},{5,7}} | collective-permute-start | bytes 2408456 | tf_op jit(solution)/shard_map/ppermute | solution.py:315
  14.0 51.6 %collective-permute-start.6 = (bf16[1536,256]{1,0:T(8,128)(2,1)}, bf16[1536,256]{1,0:T(8,128)(2,1)S(1)}, u32[]{:S(2)}, u32[]{:S(2)}) collective-permute-start(bf16[1536,256]{1,0:T(8,128)(2,1)} %get-tuple-element.35), channel_id=1, source_target_pairs={{0,2},{1,3},{4,6},{5,7}} | collective-permute-start | bytes 2359304 | tf_op jit(solution)/shard_map/ppermute | solution.py:315
  31.6 50.9 %collective-permute-start.5 = (bf16[1536,256]{1,0:T(8,128)(2,1)}, bf16[1536,256]{1,0:T(8,128)(2,1)S(1)}, u32[]{:S(2)}, u32[]{:S(2)}) collective-permute-start(bf16[1536,256]{1,0:T(8,128)(2,1)} %get-tuple-element.34), channel_id=1, source_target_pairs={{0,2},{1,3},{4,6},{5,7}} | collective-permute-start | bytes 2359304 | tf_op jit(solution)/shard_map/ppermute | solution.py:315
  32.9 0.8 copy-start
  33.7 65.6 %collective-permute-start.4 = (bf16[1536,256]{1,0:T(8,128)(2,1)}, bf16[1536,256]{1,0:T(8,128)(2,1)S(1)}, u32[]{:S(2)}, u32[]{:S(2)}) collective-permute-start(bf16[1536,256]{1,0:T(8,128)(2,1)} %get-tuple-element.33), channel_id=1, source_target_pairs={{0,2},{1,3},{4,6},{5,7}} | collective-permute-start | bytes 2359304 | tf_op jit(solution)/shard_map/ppermute | solution.py:315
  43.9 1.1 copy-start.1
  135.6 8.3 %copy-start.2 = (bf16[1280,256]{1,0:T(8,128)(2,1)S(1)}, bf16[1280,256]{1,0:T(8,128)(2,1)}, u32[]{:S(2)}) copy-start(bf16[1280,256]{1,0:T(8,128)(2,1)} %copy-done) | copy-start | bytes 1966084

commit v2 on v1

--- a/solution.py
+++ b/solution.py
@@ -8,7 +8,7 @@
 from jax.sharding import PartitionSpec as P
 
 
-CHUNKS = (6, 6, 6, 6, 5, 3)
+CHUNKS = (5, 6, 6, 5, 4, 3, 3)
 BOUNDS = tuple(sum(CHUNKS[:n]) for n in range(len(CHUNKS) + 1))
 GROUP = 2
 DEPTH = 3
@@ -69,7 +69,9 @@
     if not first:
         _, lse_in, q_in, kv_in, *rest = rest
     o_ref, lse_ref, *rest = rest
-    if not last:
+    if last:
+        lse_out, (lse_ref, lse_sem, *rest) = lse_ref, rest
+    else:
         q_out, kv_out, *rest = rest
     s_ref, n_ref, q_buf, k_buf, v_buf, o_buf, s_sem, kv_sem, q_sem, o_sem, ahead_sem = rest
     depth, heads, piece, head = q_buf.shape
@@ -219,7 +221,11 @@
 
         n_ref[0] = s_ref[jnp.minimum(base + step + 1, batch - 1)]
 
-    if not last:
+    if last:
+        log_store = pltpu.make_async_copy(lse_ref, lse_out, lse_sem)
+        log_store.start()
+        log_store.wait()
+    else:
         for copy in aheads():
             copy.wait()
     for step in range(max(size - 2, 0), size):
@@ -253,8 +259,8 @@
     return pl.pallas_call(
         functools.partial(attend_kernel, first, last, base, size),
         in_specs=in_specs,
-        out_specs=[hbm] + [vmem] * (len(out_shape) - 1),
-        scratch_shapes=[
+        out_specs=[hbm, hbm] if last else [hbm] + [vmem] * 3,
+        scratch_shapes=([pltpu.VMEM(out_shape[1].shape, jnp.float32), pltpu.SemaphoreType.DMA] if last else []) + [
             pltpu.SMEM(needs.shape, jnp.int32),
             pltpu.SMEM((1,), jnp.int32),
             pltpu.VMEM((DEPTH, heads, piece, head), jnp.bfloat16),
@@ -269,7 +275,7 @@
         ],
         out_shape=out_shape,
         input_output_aliases=aliases,
-        compiler_params=pltpu.CompilerParams(vmem_limit_bytes=32 << 20),
+        compiler_params=pltpu.CompilerParams(vmem_limit_bytes=20 << 20),
         cost_estimate=pl.CostEstimate(
             flops=size * heads * piece * 4 * piece * head * 4,
             bytes_accessed=size * heads * piece * head * 4,

time: 157 us -> 163 us (1.038)
  waiting for transfers between devices: 49.7 us -> 64.9 us
  Pallas kernels: 92.3 us -> 80.7 us
    ppermute x7 -> x8, waiting for transfers between devices: 49.7 us -> 64.9 us  [shift(): return lax.ppermute(x, 'cp', pairs)]
    pallas_call x6 -> x7, Pallas kernels: 37.9 us -> 25 us  [swap(): pl.pallas_call(swap_kernel, in_specs=[vmem], out_specs=vmem, out_shape=ja...]
    pallas_call x6 -> x7, Pallas kernels: 46.2 us -> 47.6 us  [attend(): pl.pallas_call(functools.partial(attend_kernel, first, last, base, size),...]
    ppermute x7 -> x8, starting transfers between devices: 9.02 us -> 10.3 us  [shift(): return lax.ppermute(x, 'cp', pairs)]
  transfers between devices with their start and end apart: 7 -> 8, of which waited for: 4 -> 3; matrix products, arithmetic and copies ran while one was open for 0% -> 0% of each run, Pallas kernels for 26% -> 17%
where the time goes in v2:
time: 163 us; the launch traced here: 161 us
  Pallas kernels  80.7 us (50%)
  waiting for transfers between devices  64.9 us (40%)
  starting transfers between devices  10.3 us (6%)
  local copies, waits for them, and re-layouts  2.81 us (2%)
    ppermute x8, waiting for transfers between devices, shift(): return lax.ppermute(x, 'cp', pairs)  64.9 us
    pallas_call x7, Pallas kernels, attend(): pl.pallas_call(functools.partial(attend_kernel, first, last, base, size),...  47.6 us
    pallas_call x7, Pallas kernels, swap(): pl.pallas_call(swap_kernel, in_specs=[vmem], out_specs=vmem, out_shape=ja...  25 us
    ppermute x8, starting transfers between devices, shift(): return lax.ppermute(x, 'cp', pairs)  10.3 us
    pallas_call x2, Pallas kernels, pack(): pl.pallas_call(functools.partial(pack_kernel, ranges, tails), in_specs=[h...  8.08 us
  transfers between devices with their start and end apart: 8, of which 3 were waited for; matrix products, arithmetic and copies ran while one was open for 0% of the time, Pallas kernels for 17%

profile of v2, /device:TPU:7, one launch (start us, length us, event | category | flops | bytes accessed | tf_op | source)
XLA Modules:
  0.0 161.2 jit_solution(18067527910972611584)
XLA Ops:
  0.6 6.1 %shard_map.59 = (bf16[1536,256]{1,0:T(8,128)(2,1)}, bf16[1536,256]{1,0:T(8,128)(2,1)}, bf16[1280,256]{1,0:T(8,128)(2,1)}, bf16[1024,256]{1,0:T(8,128)(2,1)S(1)},...) custom-call(s32[32,128]{1,0:T(8,128)} %seg_ref.3, ...), custom_call_target="tpu_custom_call" | custom-call | flops 1048576 | bytes 4194304 | tf_op jit(solution)/shard_map/pallas_call | solution.py:54
  6.7 1.3 collective-permute-start
  8.0 1.3 collective-permute-start.4
  9.3 1.3 collective-permute-start.3
  10.6 1.3 collective-permute-start.2
  11.9 1.3 collective-permute-start.7
  13.2 15.5 %collective-permute-done.3.mine_ref.fara_ref = bf16[768,256]{1,0:T(8,128)(2,1)S(1)} collective-permute-done((bf16[768,256]{1,0:T(8,128)(2,1)S(1)}, bf16[768,256]{1,0:T(8,128)(2,1)S(1)}, u32[]{:S(2)}, u32[]{:S(2)}) %collective-permute-start.3) | collective-permute-done | bytes 393248 | tf_op jit(solution)/shard_map/ppermute | solution.py:321
  28.7 0.0 copy-start.3
  28.7 1.3 collective-permute-start.6
  30.0 2.0 %shard_map.60 = bf16[1312,256]{1,0:T(8,128)(2,1)} custom-call(s32[32,128]{1,0:T(8,128)} %seg_ref.3, bf16[32,128,256]{2,1,0:T(8,128)(2,1)} %k_ref.17, bf16[32,128,256]{2,1,0:T(8,128)(2,1)} %v_ref.17), custom_call_target="tpu_custom_call" | custom-call | flops 1048576 | bytes 4194304 | tf_op jit(solution)/shard_map/pallas_call | solution.py:54
  32.0 0.0 copy-done.3
  32.1 5.1 %collective-permute-done.2.mine_ref.fara_ref = bf16[768,256]{1,0:T(8,128)(2,1)S(1)} collective-permute-done((bf16[768,256]{1,0:T(8,128)(2,1)S(1)}, bf16[768,256]{1,0:T(8,128)(2,1)S(1)}, u32[]{:S(2)}, u32[]{:S(2)}) %collective-permute-start.2) | collective-permute-done | bytes 393248 | tf_op jit(solution)/shard_map/ppermute | solution.py:321
  37.2 0.0 copy-start
  37.2 0.7 copy-done
  37.9 1.3 collective-permute-start.1
  39.2 0.0 collective-permute-done.4.mine_ref.fara_ref
  39.2 1.3 collective-permute-start.5
  40.5 0.0 copy-start.4
  40.5 1.0 copy-done.4
  41.5 8.8 %shard_map.63.farb_ref = bf16[768,256]{1,0:T(8,128)(2,1)S(1)} custom-call(bf16[768,256]{1,0:T(8,128)(2,1)S(1)} %copy-done.4), custom_call_target="tpu_custom_call" | custom-call | flops 1048576 | bytes 786432 | tf_op jit(solution)/shard_map/pallas_call | solution.py:307
  50.4 0.0 copy-start.1
  50.4 1.0 copy-done.1
  51.4 1.7 %shard_map.62.farb_ref = bf16[768,256]{1,0:T(8,128)(2,1)S(1)} custom-call(bf16[768,256]{1,0:T(8,128)(2,1)S(1)} %copy-done.1), custom_call_target="tpu_custom_call" | custom-call | flops 1048576 | bytes 786432 | tf_op jit(solution)/shard_map/pallas_call | solution.py:307
  53.1 1.9 %shard_map.64.farb_ref = bf16[1024,256]{1,0:T(8,128)(2,1)S(1)} custom-call(bf16[1024,256]{1,0:T(8,128)(2,1)S(1)} %collective-permute-done.4.mine_ref.fara_ref), custom_call_target="tpu_custom_call" | custom-call | flops 1048576 | bytes 1048576 | tf_op jit(solution)/shard_map/pallas_call | solution.py:307
  55.1 44.3 %collective-permute-done.5.mine_ref.fara_ref = bf16[1280,256]{1,0:T(8,128)(2,1)S(1)} collective-permute-done((bf16[1280,256]{1,0:T(8,128)(2,1)}, bf16[1280,256]{1,0:T(8,128)(2,1)S(1)}, u32[]{:S(2)}, u32[]{:S(2)}) %collective-permute-start.5) | collective-permute-done | bytes 655392 | tf_op jit(solution)/shard_map/ppermute | solution.py:321
  99.3 5.7 %shard_map.65.farb_ref = bf16[1280,256]{1,0:T(8,128)(2,1)S(1)} custom-call(bf16[1280,256]{1,0:T(8,128)(2,1)S(1)} %collective-permute-done.5.mine_ref.fara_ref), custom_call_target="tpu_custom_call" | custom-call | flops 1048576 | bytes 1310720 | tf_op jit(solution)/shard_map/pallas_call | solution.py:307
  105.0 0.0 collective-permute-done.1.mine_ref.fara_ref
  105.0 2.2 %shard_map.61.farb_ref = bf16[1312,256]{1,0:T(8,128)(2,1)S(1)} custom-call(bf16[1312,256]{1,0:T(8,128)(2,1)S(1)} %collective-permute-done.1.mine_ref.fara_ref), custom_call_target="tpu_custom_call" | custom-call | flops 1048576 | bytes 1343488 | tf_op jit(solution)/shard_map/pallas_call | solution.py:307
  107.2 0.0 collective-permute-done.7.mine_ref.fara_ref
  107.2 2.3 %shard_map.67.farb_ref = bf16[1536,256]{1,0:T(8,128)(2,1)S(1)} custom-call(bf16[1536,256]{1,0:T(8,128)(2,1)S(1)} %collective-permute-done.7.mine_ref.fara_ref), custom_call_target="tpu_custom_call" | custom-call | flops 1048576 | bytes 1572864 | tf_op jit(solution)/shard_map/pallas_call | solution.py:307
  109.5 0.0 collective-permute-done.6.mine_ref.fara_ref
  109.5 2.3 %shard_map.66.farb_ref = bf16[1536,256]{1,0:T(8,128)(2,1)S(1)} custom-call(bf16[1536,256]{1,0:T(8,128)(2,1)S(1)} %collective-permute-done.6.mine_ref.fara_ref), custom_call_target="tpu_custom_call" | custom-call | flops 1048576 | bytes 1572864 | tf_op jit(solution)/shard_map/pallas_call | solution.py:307
  111.8 0.0 collective-permute-done.near_ref
  111.9 0.8 subtract_reduce_fusion
  112.7 0.5 fusion.s_hbm
  113.2 0.1 broadcast_in_dim.23.cut_ref
  113.3 8.5 %shard_map.68 = (bf16[32,10,128,256]{3,2,1,0:T(8,128)(2,1)}, f32[10,32,128]{2,1,0:T(8,128)S(1)}, bf16[10,128,256]{2,1,0:T(8,128)(2,1)S(1)}, bf16[4,128,256]{2,1,0:T(8,128)(2,1)S(1)}) custom-call(s32[32]{0:T(128)} %fusion.s_hbm, s32[32,128]{1,0:T(8,128)S(1)} %broadcast_in_dim.23.cut_ref, bf16[32,10,128,256]{3,2,1,0:T(8,128)(2,1)} %bitcast.3, ...), custom_call_target="tpu_custom_call" | custom-call | flops 3355443200 | bytes 6553600 | tf_op jit(solution)/shard_map/pallas_call | solution.py:259
  121.9 8.9 %shard_map.69 = (bf16[32,10,128,256]{3,2,1,0:T(8,128)(2,1)}, f32[10,32,128]{2,1,0:T(8,128)S(1)}, bf16[10,128,256]{2,1,0:T(8,128)(2,1)S(1)}, bf16[4,128,256]{2,1,0:T(8,128)(2,1)S(1)}) custom-call(s32[32]{0:T(128)} %fusion.s_hbm, s32[32,128]{1,0:T(8,128)S(1)} %broadcast_in_dim.23.cut_ref, ...), custom_call_target="tpu_custom_call", output_to_operand_aliasing={{0}: (8, {})} | custom-call | flops 4026531840 | bytes 7864320 | tf_op jit(solution)/shard_map/pallas_call | solution.py:259
  130.8 7.8 %shard_map.70 = (bf16[32,10,128,256]{3,2,1,0:T(8,128)(2,1)}, f32[10,32,128]{2,1,0:T(8,128)S(1)}, bf16[10,128,256]{2,1,0:T(8,128)(2,1)S(1)}, bf16[4,128,256]{2,1,0:T(8,128)(2,1)S(1)}) custom-call(s32[32]{0:T(128)} %fusion.s_hbm, s32[32,128]{1,0:T(8,128)S(1)} %broadcast_in_dim.23.cut_ref, ...), custom_call_target="tpu_custom_call", output_to_operand_aliasing={{0}: (8, {})} | custom-call | flops 4026531840 | bytes 7864320 | tf_op jit(solution)/shard_map/pallas_call | solution.py:259
  138.6 7.2 %shard_map.71 = (bf16[32,10,128,256]{3,2,1,0:T(8,128)(2,1)}, f32[10,32,128]{2,1,0:T(8,128)S(1)}, bf16[10,128,256]{2,1,0:T(8,128)(2,1)S(1)}, bf16[4,128,256]{2,1,0:T(8,128)(2,1)S(1)}) custom-call(s32[32]{0:T(128)} %fusion.s_hbm, s32[32,128]{1,0:T(8,128)S(1)} %broadcast_in_dim.23.cut_ref, ...), custom_call_target="tpu_custom_call", output_to_operand_aliasing={{0}: (8, {})} | custom-call | flops 3355443200 | bytes 6553600 | tf_op jit(solution)/shard_map/pallas_call | solution.py:259
  145.8 0.0 copy-start.5
  145.9 6.2 %shard_map.72 = (bf16[32,10,128,256]{3,2,1,0:T(8,128)(2,1)}, f32[10,32,128]{2,1,0:T(8,128)S(1)}, bf16[10,128,256]{2,1,0:T(8,128)(2,1)S(1)}, bf16[4,128,256]{2,1,0:T(8,128)(2,1)S(1)}) custom-call(s32[32]{0:T(128)} %fusion.s_hbm, s32[32,128]{1,0:T(8,128)S(1)} %broadcast_in_dim.23.cut_ref, ...), custom_call_target="tpu_custom_call", output_to_operand_aliasing={{0}: (8, {})} | custom-call | flops 2684354560 | bytes 5242880 | tf_op jit(solution)/shard_map/pallas_call | solution.py:259
  152.0 0.0 copy-done.5
  152.0 0.0 copy-start.2
  152.0 4.5 %shard_map.73 = (bf16[32,10,128,256]{3,2,1,0:T(8,128)(2,1)}, f32[10,32,128]{2,1,0:T(8,128)S(1)}, bf16[10,128,256]{2,1,0:T(8,128)(2,1)S(1)}, bf16[4,128,256]{2,1,0:T(8,128)(2,1)S(1)}) custom-call(s32[32]{0:T(128)} %fusion.s_hbm, s32[32,128]{1,0:T(8,128)S(1)} %broadcast_in_dim.23.cut_ref, ...), custom_call_target="tpu_custom_call", output_to_operand_aliasing={{0}: (8, {})} | custom-call | flops 2013265920 | bytes 3932160 | tf_op jit(solution)/shard_map/pallas_call | solution.py:259
  156.6 0.0 copy-done.2
  156.6 4.5 %shard_map.74 = (bf16[32,10,128,256]{3,2,1,0:T(8,128)(2,1)}, f32[10,32,128]{2,1,0:T(8,128)}) custom-call(s32[32]{0:T(128)} %fusion.s_hbm, s32[32,128]{1,0:T(8,128)S(1)} %broadcast_in_dim.23.cut_ref, bf16[32,10,128,256]{3,2,1,0:T(8,128)(2,1)} %bitcast.9, bf16[32,128,256]{2,1,0:T(8,128)(2,1)} %k_ref.17, ...), custom_call_target="tpu_custom_call", output_to_operand_aliasing={{0}: (8, {})} | custom-call | flops 2013265920 | bytes 3932160 | tf_op jit(solution)/shard_map/pallas_call | solution.py:259
Async XLA Ops:
  6.7 105.1 %collective-permute-start = (bf16[8224,256]{1,0:T(8,128)(2,1)}, bf16[8224,256]{1,0:T(8,128)(2,1)}, u32[]{:S(2)}, u32[]{:S(2)}) collective-permute-start(bf16[8224,256]{1,0:T(8,128)(2,1)} %get-tuple-element.35), channel_id=1, source_target_pairs={{0,1},{2,3},{4,5},{6,7}} | collective-permute-start | bytes 12632072 | tf_op jit(solution)/shard_map/ppermute | solution.py:321
  8.0 31.2 %collective-permute-start.4 = (bf16[1024,256]{1,0:T(8,128)(2,1)S(1)}, bf16[1024,256]{1,0:T(8,128)(2,1)S(1)}, u32[]{:S(2)}, u32[]{:S(2)}) collective-permute-start(bf16[1024,256]{1,0:T(8,128)(2,1)S(1)} %get-tuple-element.38), channel_id=1, source_target_pairs={{0,2},{1,3},{4,6},{5,7}} | collective-permute-start | bytes 1572872 | tf_op jit(solution)/shard_map/ppermute | solution.py:321
  9.3 19.4 %collective-permute-start.3 = (bf16[768,256]{1,0:T(8,128)(2,1)S(1)}, bf16[768,256]{1,0:T(8,128)(2,1)S(1)}, u32[]{:S(2)}, u32[]{:S(2)}) collective-permute-start(bf16[768,256]{1,0:T(8,128)(2,1)S(1)} %get-tuple-element.37), channel_id=1, source_target_pairs={{0,2},{1,3},{4,6},{5,7}} | collective-permute-start | bytes 1179656 | tf_op jit(solution)/shard_map/ppermute | solution.py:321
  10.6 26.6 %collective-permute-start.2 = (bf16[768,256]{1,0:T(8,128)(2,1)S(1)}, bf16[768,256]{1,0:T(8,128)(2,1)S(1)}, u32[]{:S(2)}, u32[]{:S(2)}) collective-permute-start(bf16[768,256]{1,0:T(8,128)(2,1)S(1)} %get-tuple-element.36), channel_id=1, source_target_pairs={{0,2},{1,3},{4,6},{5,7}} | collective-permute-start | bytes 1179656 | tf_op jit(solution)/shard_map/ppermute | solution.py:321
  11.9 95.3 %collective-permute-start.7 = (bf16[1536,256]{1,0:T(8,128)(2,1)}, bf16[1536,256]{1,0:T(8,128)(2,1)S(1)}, u32[]{:S(2)}, u32[]{:S(2)}) collective-permute-start(bf16[1536,256]{1,0:T(8,128)(2,1)} %get-tuple-element.41), channel_id=1, source_target_pairs={{0,2},{1,3},{4,6},{5,7}} | collective-permute-start | bytes 2359304 | tf_op jit(solution)/shard_map/ppermute | solution.py:321
  28.7 3.3 %copy-start.3 = (bf16[768,256]{1,0:T(8,128)(2,1)}, bf16[768,256]{1,0:T(8,128)(2,1)S(1)}, u32[]{:S(2)}) copy-start(bf16[768,256]{1,0:T(8,128)(2,1)S(1)} %collective-permute-done.3.mine_ref.fara_ref) | copy-start | bytes 1179652
  28.7 80.8 %collective-permute-start.6 = (bf16[1536,256]{1,0:T(8,128)(2,1)}, bf16[1536,256]{1,0:T(8,128)(2,1)S(1)}, u32[]{:S(2)}, u32[]{:S(2)}) collective-permute-start(bf16[1536,256]{1,0:T(8,128)(2,1)} %get-tuple-element.40), channel_id=1, source_target_pairs={{0,2},{1,3},{4,6},{5,7}} | collective-permute-start | bytes 2359304 | tf_op jit(solution)/shard_map/ppermute | solution.py:321
  37.2 0.7 copy-start
  37.9 67.1 %collective-permute-start.1 = (bf16[1312,256]{1,0:T(8,128)(2,1)}, bf16[1312,256]{1,0:T(8,128)(2,1)S(1)}, u32[]{:S(2)}, u32[]{:S(2)}) collective-permute-start(bf16[1312,256]{1,0:T(8,128)(2,1)} %shard_map.60), channel_id=1, source_target_pairs={{0,2},{1,3},{4,6},{5,7}} | collective-permute-start | bytes 2015240 | tf_op jit(solution)/shard_map/ppermute | solution.py:321
  39.2 60.1 %collective-permute-start.5 = (bf16[1280,256]{1,0:T(8,128)(2,1)}, bf16[1280,256]{1,0:T(8,128)(2,1)S(1)}, u32[]{:S(2)}, u32[]{:S(2)}) collective-permute-start(bf16[1280,256]{1,0:T(8,128)(2,1)} %get-tuple-element.39), channel_id=1, source_target_pairs={{0,2},{1,3},{4,6},{5,7}} | collective-permute-start | bytes 1966088 | tf_op jit(solution)/shard_map/ppermute | solution.py:321
  40.5 1.0 copy-start.4
  50.4 1.0 copy-start.1
  145.8 6.2 %copy-start.5 = (bf16[768,256]{1,0:T(8,128)(2,1)S(1)}, bf16[768,256]{1,0:T(8,128)(2,1)}, u32[]{:S(2)}) copy-start(bf16[768,256]{1,0:T(8,128)(2,1)} %copy-done.3) | copy-start | bytes 1179652
  152.0 4.5 %copy-start.2 = (bf16[768,256]{1,0:T(8,128)(2,1)S(1)}, bf16[768,256]{1,0:T(8,128)(2,1)}, u32[]{:S(2)}) copy-start(bf16[768,256]{1,0:T(8,128)(2,1)} %copy-done) | copy-start | bytes 1179652

commit v3 on v2

--- a/solution.py
+++ b/solution.py
@@ -18,48 +18,63 @@
 BESIDE = [(0, 1), (2, 3)]
 
 
-def pack_kernel(ranges, tails, seg_ref, k_ref, v_ref, *rest):
-    outs, (seg_scr, seg_sem, sem) = rest[:-3], rest[-3:]
+def pack_kernel(senders, ranges, tails, seg_ref, k_ref, v_ref, *rest):
+    count = len(ranges)
+    outs, (seg_scr, seg_sem, sem, *stages) = rest[:count], rest[count:]
+    finals, outs = (outs, stages) if stages else ((), outs)
     batch, piece, head = k_ref.shape
     segments = pltpu.make_async_copy(seg_ref, seg_scr, seg_sem)
-    segments.start()
 
     def copies(i, out, at):
         for half, ref in enumerate((k_ref, v_ref)):
             rows = pl.ds(pl.multiple_of((2 * i + half) * piece, piece), piece)
             yield pltpu.make_async_copy(ref.at[at + i], out.at[rows], sem)
 
-    for out, (a, b) in zip(outs, ranges):
-        @pl.loop(0, b - a)
-        def _(i):
-            for copy in copies(i, out, a):
-                copy.start()
-    segments.wait()
-    here = jnp.sum((seg_scr[...] == 0).astype(jnp.float32), axis=1, keepdims=True)
-    rows = jnp.broadcast_to(here, (batch, head)).astype(jnp.bfloat16)
-    for out, (a, b), tail in zip(outs, ranges, tails):
-        if tail:
-            out[(b - a) * 2 * piece:] = rows
-    for out, (a, b) in zip(outs, ranges):
-        @pl.loop(0, b - a)
-        def _(i):
-            for copy in copies(i, out, a):
-                copy.wait()
-
-
-def pack(ranges, tails, seg, k, v):
+    def fill():
+        segments.start()
+        for out, (a, b) in zip(outs, ranges):
+            @pl.loop(0, b - a)
+            def _(i):
+                for copy in copies(i, out, a):
+                    copy.start()
+        segments.wait()
+        here = jnp.sum((seg_scr[...] == 0).astype(jnp.float32), axis=1, keepdims=True)
+        rows = jnp.broadcast_to(here, (batch, head)).astype(jnp.bfloat16)
+        for out, (a, b), tail in zip(outs, ranges, tails):
+            if tail:
+                out[(b - a) * 2 * piece:] = rows
+        for out, (a, b) in zip(outs, ranges):
+            @pl.loop(0, b - a)
+            def _(i):
+                for copy in copies(i, out, a):
+                    copy.wait()
+        stores = [pltpu.make_async_copy(out, final, sem) for out, final in zip(outs, finals)]
+        for store in stores:
+            store.start()
+        for store in stores:
+            store.wait()
+
+    if senders is None:
+        fill()
+    else:
+        pl.when(lax.axis_index("cp") < senders)(fill)
+
+
+def pack(senders, ranges, tails, seg, k, v):
     batch, piece, head = k.shape
     vmem, hbm = pl.BlockSpec(memory_space=pltpu.VMEM), pl.BlockSpec(memory_space=pltpu.HBM)
     seg, k, v = (pltpu.with_memory_space_constraint(x, pltpu.HBM) for x in (seg, k, v))
+    out_shape = [
+        jax.ShapeDtypeStruct(((b - a) * 2 * piece + (batch if tail else 0), head), jnp.bfloat16)
+        for (a, b), tail in zip(ranges, tails)
+    ]
+    stages = [] if senders is None else [pltpu.VMEM(x.shape, x.dtype) for x in out_shape]
     return pl.pallas_call(
-        functools.partial(pack_kernel, ranges, tails),
+        functools.partial(pack_kernel, senders, ranges, tails),
         in_specs=[hbm] * 3,
-        out_specs=[vmem] * len(ranges),
-        out_shape=[
-            jax.ShapeDtypeStruct(((b - a) * 2 * piece + (batch if tail else 0), head), jnp.bfloat16)
-            for (a, b), tail in zip(ranges, tails)
-        ],
-        scratch_shapes=[pltpu.VMEM(seg.shape, jnp.int32), pltpu.SemaphoreType.DMA, pltpu.SemaphoreType.DMA],
+        out_specs=[hbm if stages else vmem] * len(ranges),
+        out_shape=out_shape,
+        scratch_shapes=[pltpu.VMEM(seg.shape, jnp.int32), pltpu.SemaphoreType.DMA, pltpu.SemaphoreType.DMA] + stages,
         compiler_params=pltpu.CompilerParams(vmem_limit_bytes=16 << 20),
         cost_estimate=pl.CostEstimate(flops=1 << 20, bytes_accessed=4 * k.size, transcendentals=0),
     )(seg, k, v)
@@ -327,8 +342,8 @@
         me = lax.axis_index("cp")
         q = jnp.transpose(q_loc, (0, 2, 1, 3))
         ranges = tuple(zip(BOUNDS[:-1], BOUNDS[1:]))
-        sends = pack(ranges[:1], (True,), seg_loc, k_loc, v_loc)
-        *more, whole = pack(ranges[1:] + ((0, batch),), (False,) * len(ranges[1:]) + (True,), seg_loc, k_loc, v_loc)
+        sends = pack(2, ranges[:1], (True,), seg_loc, k_loc, v_loc)
+        *more, whole = pack(None, ranges[1:] + ((0, batch),), (False,) * len(ranges[1:]) + (True,), seg_loc, k_loc, v_loc)
         sends = list(sends) + more
         fara = [shift(x, ACROSS) for x in sends]
         near = shift(whole, BESIDE)

time: 163 us -> 163 us (level)
  Pallas kernels: 80.7 us -> 78.7 us
  waiting for transfers between devices: 64.9 us -> 66.9 us
    ppermute x8, waiting for transfers between devices: 64.9 us -> 66.9 us  [shift(): return lax.ppermute(x, 'cp', pairs)]
    pallas_call x2, Pallas kernels: 8.08 us -> 6.12 us  [pack(): pl.pallas_call(functools.partial(pack_kernel, senders, ranges, tails), in...]
  transfers between devices with their start and end apart: 8 -> 8, of which waited for: 3 -> 3; matrix products, arithmetic and copies ran while one was open for 0% -> 0% of each run, Pallas kernels for 17% -> 16%
where the time goes in v3:
time: 163 us; the launch traced here: 161 us
  Pallas kernels  78.7 us (48%)
  waiting for transfers between devices  66.9 us (41%)
  starting transfers between devices  10.3 us (6%)
  local copies, waits for them, and re-layouts  2.81 us (2%)
    ppermute x8, waiting for transfers between devices, shift(): return lax.ppermute(x, 'cp', pairs)  66.9 us
    pallas_call x7, Pallas kernels, attend(): pl.pallas_call(functools.partial(attend_kernel, first, last, base, size),...  47.6 us
    pallas_call x7, Pallas kernels, swap(): pl.pallas_call(swap_kernel, in_specs=[vmem], out_specs=vmem, out_shape=ja...  25 us
    ppermute x8, starting transfers between devices, shift(): return lax.ppermute(x, 'cp', pairs)  10.3 us
    pallas_call x2, Pallas kernels, pack(): pl.pallas_call(functools.partial(pack_kernel, senders, ranges, tails), in...  6.12 us
  transfers between devices with their start and end apart: 8, of which 3 were waited for; matrix products, arithmetic and copies ran while one was open for 0% of the time, Pallas kernels for 16%

profile of v3, /device:TPU:7, one launch (start us, length us, event | category | flops | bytes accessed | tf_op | source)
XLA Modules:
  0.0 161.2 jit_solution(11214643859108349694)
XLA Ops:
  0.6 6.1 %shard_map.59 = (bf16[1536,256]{1,0:T(8,128)(2,1)}, bf16[1536,256]{1,0:T(8,128)(2,1)}, bf16[1280,256]{1,0:T(8,128)(2,1)}, bf16[1024,256]{1,0:T(8,128)(2,1)S(1)},...) custom-call(s32[32,128]{1,0:T(8,128)} %seg_ref.3, ...), custom_call_target="tpu_custom_call" | custom-call | flops 1048576 | bytes 4194304 | tf_op jit(solution)/shard_map/pallas_call | solution.py:72
  6.7 1.3 collective-permute-start
  8.0 1.3 collective-permute-start.4
  9.3 1.3 collective-permute-start.3
  10.6 1.3 collective-permute-start.2
  11.9 1.3 collective-permute-start.7
  13.2 15.5 %collective-permute-done.3.mine_ref.fara_ref = bf16[768,256]{1,0:T(8,128)(2,1)S(1)} collective-permute-done((bf16[768,256]{1,0:T(8,128)(2,1)S(1)}, bf16[768,256]{1,0:T(8,128)(2,1)S(1)}, u32[]{:S(2)}, u32[]{:S(2)}) %collective-permute-start.3) | collective-permute-done | bytes 393248 | tf_op jit(solution)/shard_map/ppermute | solution.py:336
  28.7 0.0 copy-start.3
  28.7 1.3 collective-permute-start.6
  30.1 0.0 copy-done.3
  30.1 7.1 %collective-permute-done.2.mine_ref.fara_ref = bf16[768,256]{1,0:T(8,128)(2,1)S(1)} collective-permute-done((bf16[768,256]{1,0:T(8,128)(2,1)S(1)}, bf16[768,256]{1,0:T(8,128)(2,1)S(1)}, u32[]{:S(2)}, u32[]{:S(2)}) %collective-permute-start.2) | collective-permute-done | bytes 393248 | tf_op jit(solution)/shard_map/ppermute | solution.py:336
  37.2 0.0 copy-start
  37.2 0.7 copy-done
  37.9 1.3 collective-permute-start.1
  39.2 0.0 collective-permute-done.4.mine_ref.fara_ref
  39.2 1.3 collective-permute-start.5
  40.5 0.0 copy-start.4
  40.5 1.0 copy-done.4
  41.5 8.8 %shard_map.63.farb_ref = bf16[768,256]{1,0:T(8,128)(2,1)S(1)} custom-call(bf16[768,256]{1,0:T(8,128)(2,1)S(1)} %copy-done.4), custom_call_target="tpu_custom_call" | custom-call | flops 1048576 | bytes 786432 | tf_op jit(solution)/shard_map/pallas_call | solution.py:322
  50.4 0.0 copy-start.1
  50.4 1.0 copy-done.1
  51.4 1.7 %shard_map.62.farb_ref = bf16[768,256]{1,0:T(8,128)(2,1)S(1)} custom-call(bf16[768,256]{1,0:T(8,128)(2,1)S(1)} %copy-done.1), custom_call_target="tpu_custom_call" | custom-call | flops 1048576 | bytes 786432 | tf_op jit(solution)/shard_map/pallas_call | solution.py:322
  53.1 1.9 %shard_map.64.farb_ref = bf16[1024,256]{1,0:T(8,128)(2,1)S(1)} custom-call(bf16[1024,256]{1,0:T(8,128)(2,1)S(1)} %collective-permute-done.4.mine_ref.fara_ref), custom_call_target="tpu_custom_call" | custom-call | flops 1048576 | bytes 1048576 | tf_op jit(solution)/shard_map/pallas_call | solution.py:322
  55.1 44.3 %collective-permute-done.5.mine_ref.fara_ref = bf16[1280,256]{1,0:T(8,128)(2,1)S(1)} collective-permute-done((bf16[1280,256]{1,0:T(8,128)(2,1)}, bf16[1280,256]{1,0:T(8,128)(2,1)S(1)}, u32[]{:S(2)}, u32[]{:S(2)}) %collective-permute-start.5) | collective-permute-done | bytes 655392 | tf_op jit(solution)/shard_map/ppermute | solution.py:336
  99.3 5.7 %shard_map.65.farb_ref = bf16[1280,256]{1,0:T(8,128)(2,1)S(1)} custom-call(bf16[1280,256]{1,0:T(8,128)(2,1)S(1)} %collective-permute-done.5.mine_ref.fara_ref), custom_call_target="tpu_custom_call" | custom-call | flops 1048576 | bytes 1310720 | tf_op jit(solution)/shard_map/pallas_call | solution.py:322
  105.0 0.0 collective-permute-done.1.mine_ref.fara_ref
  105.0 2.2 %shard_map.61.farb_ref = bf16[1312,256]{1,0:T(8,128)(2,1)S(1)} custom-call(bf16[1312,256]{1,0:T(8,128)(2,1)S(1)} %collective-permute-done.1.mine_ref.fara_ref), custom_call_target="tpu_custom_call" | custom-call | flops 1048576 | bytes 1343488 | tf_op jit(solution)/shard_map/pallas_call | solution.py:322
  107.2 0.0 collective-permute-done.7.mine_ref.fara_ref
  107.2 2.3 %shard_map.67.farb_ref = bf16[1536,256]{1,0:T(8,128)(2,1)S(1)} custom-call(bf16[1536,256]{1,0:T(8,128)(2,1)S(1)} %collective-permute-done.7.mine_ref.fara_ref), custom_call_target="tpu_custom_call" | custom-call | flops 1048576 | bytes 1572864 | tf_op jit(solution)/shard_map/pallas_call | solution.py:322
  109.5 0.0 collective-permute-done.6.mine_ref.fara_ref
  109.5 2.3 %shard_map.66.farb_ref = bf16[1536,256]{1,0:T(8,128)(2,1)S(1)} custom-call(bf16[1536,256]{1,0:T(8,128)(2,1)S(1)} %collective-permute-done.6.mine_ref.fara_ref), custom_call_target="tpu_custom_call" | custom-call | flops 1048576 | bytes 1572864 | tf_op jit(solution)/shard_map/pallas_call | solution.py:322
  111.8 0.0 collective-permute-done.near_ref
  111.9 0.8 subtract_reduce_fusion
  112.7 0.5 fusion.s_hbm
  113.2 0.1 broadcast_in_dim.23.cut_ref
  113.3 8.5 %shard_map.68 = (bf16[32,10,128,256]{3,2,1,0:T(8,128)(2,1)}, f32[10,32,128]{2,1,0:T(8,128)S(1)}, bf16[10,128,256]{2,1,0:T(8,128)(2,1)S(1)}, bf16[4,128,256]{2,1,0:T(8,128)(2,1)S(1)}) custom-call(s32[32]{0:T(128)} %fusion.s_hbm, s32[32,128]{1,0:T(8,128)S(1)} %broadcast_in_dim.23.cut_ref, bf16[32,10,128,256]{3,2,1,0:T(8,128)(2,1)} %bitcast.3, ...), custom_call_target="tpu_custom_call" | custom-call | flops 3355443200 | bytes 6553600 | tf_op jit(solution)/shard_map/pallas_call | solution.py:274
  121.9 8.9 %shard_map.69 = (bf16[32,10,128,256]{3,2,1,0:T(8,128)(2,1)}, f32[10,32,128]{2,1,0:T(8,128)S(1)}, bf16[10,128,256]{2,1,0:T(8,128)(2,1)S(1)}, bf16[4,128,256]{2,1,0:T(8,128)(2,1)S(1)}) custom-call(s32[32]{0:T(128)} %fusion.s_hbm, s32[32,128]{1,0:T(8,128)S(1)} %broadcast_in_dim.23.cut_ref, ...), custom_call_target="tpu_custom_call", output_to_operand_aliasing={{0}: (8, {})} | custom-call | flops 4026531840 | bytes 7864320 | tf_op jit(solution)/shard_map/pallas_call | solution.py:274
  130.8 7.8 %shard_map.70 = (bf16[32,10,128,256]{3,2,1,0:T(8,128)(2,1)}, f32[10,32,128]{2,1,0:T(8,128)S(1)}, bf16[10,128,256]{2,1,0:T(8,128)(2,1)S(1)}, bf16[4,128,256]{2,1,0:T(8,128)(2,1)S(1)}) custom-call(s32[32]{0:T(128)} %fusion.s_hbm, s32[32,128]{1,0:T(8,128)S(1)} %broadcast_in_dim.23.cut_ref, ...), custom_call_target="tpu_custom_call", output_to_operand_aliasing={{0}: (8, {})} | custom-call | flops 4026531840 | bytes 7864320 | tf_op jit(solution)/shard_map/pallas_call | solution.py:274
  138.6 7.2 %shard_map.71 = (bf16[32,10,128,256]{3,2,1,0:T(8,128)(2,1)}, f32[10,32,128]{2,1,0:T(8,128)S(1)}, bf16[10,128,256]{2,1,0:T(8,128)(2,1)S(1)}, bf16[4,128,256]{2,1,0:T(8,128)(2,1)S(1)}) custom-call(s32[32]{0:T(128)} %fusion.s_hbm, s32[32,128]{1,0:T(8,128)S(1)} %broadcast_in_dim.23.cut_ref, ...), custom_call_target="tpu_custom_call", output_to_operand_aliasing={{0}: (8, {})} | custom-call | flops 3355443200 | bytes 6553600 | tf_op jit(solution)/shard_map/pallas_call | solution.py:274
  145.8 0.0 copy-start.5
  145.9 6.2 %shard_map.72 = (bf16[32,10,128,256]{3,2,1,0:T(8,128)(2,1)}, f32[10,32,128]{2,1,0:T(8,128)S(1)}, bf16[10,128,256]{2,1,0:T(8,128)(2,1)S(1)}, bf16[4,128,256]{2,1,0:T(8,128)(2,1)S(1)}) custom-call(s32[32]{0:T(128)} %fusion.s_hbm, s32[32,128]{1,0:T(8,128)S(1)} %broadcast_in_dim.23.cut_ref, ...), custom_call_target="tpu_custom_call", output_to_operand_aliasing={{0}: (8, {})} | custom-call | flops 2684354560 | bytes 5242880 | tf_op jit(solution)/shard_map/pallas_call | solution.py:274
  152.0 0.0 copy-done.5
  152.0 0.0 copy-start.2
  152.0 4.5 %shard_map.73 = (bf16[32,10,128,256]{3,2,1,0:T(8,128)(2,1)}, f32[10,32,128]{2,1,0:T(8,128)S(1)}, bf16[10,128,256]{2,1,0:T(8,128)(2,1)S(1)}, bf16[4,128,256]{2,1,0:T(8,128)(2,1)S(1)}) custom-call(s32[32]{0:T(128)} %fusion.s_hbm, s32[32,128]{1,0:T(8,128)S(1)} %broadcast_in_dim.23.cut_ref, ...), custom_call_target="tpu_custom_call", output_to_operand_aliasing={{0}: (8, {})} | custom-call | flops 2013265920 | bytes 3932160 | tf_op jit(solution)/shard_map/pallas_call | solution.py:274
  156.6 0.0 copy-done.2
  156.6 4.5 %shard_map.74 = (bf16[32,10,128,256]{3,2,1,0:T(8,128)(2,1)}, f32[10,32,128]{2,1,0:T(8,128)}) custom-call(s32[32]{0:T(128)} %fusion.s_hbm, s32[32,128]{1,0:T(8,128)S(1)} %broadcast_in_dim.23.cut_ref, bf16[32,10,128,256]{3,2,1,0:T(8,128)(2,1)} %bitcast.9, bf16[32,128,256]{2,1,0:T(8,128)(2,1)} %k_ref.17, ...), custom_call_target="tpu_custom_call", output_to_operand_aliasing={{0}: (8, {})} | custom-call | flops 2013265920 | bytes 3932160 | tf_op jit(solution)/shard_map/pallas_call | solution.py:274
  (1 shorter events, 0.0 us)
Async XLA Ops:
  6.7 105.1 %collective-permute-start = (bf16[8224,256]{1,0:T(8,128)(2,1)}, bf16[8224,256]{1,0:T(8,128)(2,1)}, u32[]{:S(2)}, u32[]{:S(2)}) collective-permute-start(bf16[8224,256]{1,0:T(8,128)(2,1)} %get-tuple-element.35), channel_id=1, source_target_pairs={{0,1},{2,3},{4,5},{6,7}} | collective-permute-start | bytes 12632072 | tf_op jit(solution)/shard_map/ppermute | solution.py:336
  8.0 31.2 %collective-permute-start.4 = (bf16[1024,256]{1,0:T(8,128)(2,1)S(1)}, bf16[1024,256]{1,0:T(8,128)(2,1)S(1)}, u32[]{:S(2)}, u32[]{:S(2)}) collective-permute-start(bf16[1024,256]{1,0:T(8,128)(2,1)S(1)} %get-tuple-element.38), channel_id=1, source_target_pairs={{0,2},{1,3},{4,6},{5,7}} | collective-permute-start | bytes 1572872 | tf_op jit(solution)/shard_map/ppermute | solution.py:336
  9.3 19.4 %collective-permute-start.3 = (bf16[768,256]{1,0:T(8,128)(2,1)S(1)}, bf16[768,256]{1,0:T(8,128)(2,1)S(1)}, u32[]{:S(2)}, u32[]{:S(2)}) collective-permute-start(bf16[768,256]{1,0:T(8,128)(2,1)S(1)} %get-tuple-element.37), channel_id=1, source_target_pairs={{0,2},{1,3},{4,6},{5,7}} | collective-permute-start | bytes 1179656 | tf_op jit(solution)/shard_map/ppermute | solution.py:336
  10.6 26.6 %collective-permute-start.2 = (bf16[768,256]{1,0:T(8,128)(2,1)S(1)}, bf16[768,256]{1,0:T(8,128)(2,1)S(1)}, u32[]{:S(2)}, u32[]{:S(2)}) collective-permute-start(bf16[768,256]{1,0:T(8,128)(2,1)S(1)} %get-tuple-element.36), channel_id=1, source_target_pairs={{0,2},{1,3},{4,6},{5,7}} | collective-permute-start | bytes 1179656 | tf_op jit(solution)/shard_map/ppermute | solution.py:336
  11.9 95.3 %collective-permute-start.7 = (bf16[1536,256]{1,0:T(8,128)(2,1)}, bf16[1536,256]{1,0:T(8,128)(2,1)S(1)}, u32[]{:S(2)}, u32[]{:S(2)}) collective-permute-start(bf16[1536,256]{1,0:T(8,128)(2,1)} %get-tuple-element.41), channel_id=1, source_target_pairs={{0,2},{1,3},{4,6},{5,7}} | collective-permute-start | bytes 2359304 | tf_op jit(solution)/shard_map/ppermute | solution.py:336
  28.7 1.3 copy-start.3
  28.7 80.8 %collective-permute-start.6 = (bf16[1536,256]{1,0:T(8,128)(2,1)}, bf16[1536,256]{1,0:T(8,128)(2,1)S(1)}, u32[]{:S(2)}, u32[]{:S(2)}) collective-permute-start(bf16[1536,256]{1,0:T(8,128)(2,1)} %get-tuple-element.40), channel_id=1, source_target_pairs={{0,2},{1,3},{4,6},{5,7}} | collective-permute-start | bytes 2359304 | tf_op jit(solution)/shard_map/ppermute | solution.py:336
  37.2 0.7 copy-start
  37.9 67.1 %collective-permute-start.1 = (bf16[1312,256]{1,0:T(8,128)(2,1)}, bf16[1312,256]{1,0:T(8,128)(2,1)S(1)}, u32[]{:S(2)}, u32[]{:S(2)}) collective-permute-start(bf16[1312,256]{1,0:T(8,128)(2,1)} %shard_map.60), channel_id=1, source_target_pairs={{0,2},{1,3},{4,6},{5,7}} | collective-permute-start | bytes 2015240 | tf_op jit(solution)/shard_map/ppermute | solution.py:336
  39.2 60.1 %collective-permute-start.5 = (bf16[1280,256]{1,0:T(8,128)(2,1)}, bf16[1280,256]{1,0:T(8,128)(2,1)S(1)}, u32[]{:S(2)}, u32[]{:S(2)}) collective-permute-start(bf16[1280,256]{1,0:T(8,128)(2,1)} %get-tuple-element.39), channel_id=1, source_target_pairs={{0,2},{1,3},{4,6},{5,7}} | collective-permute-start | bytes 1966088 | tf_op jit(solution)/shard_map/ppermute | solution.py:336
  40.5 1.0 copy-start.4
  50.4 1.0 copy-start.1
  145.8 6.2 %copy-start.5 = (bf16[768,256]{1,0:T(8,128)(2,1)S(1)}, bf16[768,256]{1,0:T(8,128)(2,1)}, u32[]{:S(2)}) copy-start(bf16[768,256]{1,0:T(8,128)(2,1)} %copy-done.3) | copy-start | bytes 1179652
  152.0 4.5 %copy-start.2 = (bf16[768,256]{1,0:T(8,128)(2,1)S(1)}, bf16[768,256]{1,0:T(8,128)(2,1)}, u32[]{:S(2)}) copy-start(bf16[768,256]{1,0:T(8,128)(2,1)} %copy-done) | copy-start | bytes 1179652

commit v4 on v3

--- a/solution.py
+++ b/solution.py
@@ -8,7 +8,7 @@
 from jax.sharding import PartitionSpec as P
 
 
-CHUNKS = (5, 6, 6, 5, 4, 3, 3)
+CHUNKS = (4, 6, 6, 6, 4, 3, 3)
 BOUNDS = tuple(sum(CHUNKS[:n]) for n in range(len(CHUNKS) + 1))
 GROUP = 2
 DEPTH = 3
@@ -19,9 +19,7 @@
 
 
 def pack_kernel(senders, ranges, tails, seg_ref, k_ref, v_ref, *rest):
-    count = len(ranges)
-    outs, (seg_scr, seg_sem, sem, *stages) = rest[:count], rest[count:]
-    finals, outs = (outs, stages) if stages else ((), outs)
+    outs, (seg_scr, seg_sem, sem) = rest[:-3], rest[-3:]
     batch, piece, head = k_ref.shape
     segments = pltpu.make_async_copy(seg_ref, seg_scr, seg_sem)
 
@@ -48,11 +46,6 @@
             def _(i):
                 for copy in copies(i, out, a):
                     copy.wait()
-        stores = [pltpu.make_async_copy(out, final, sem) for out, final in zip(outs, finals)]
-        for store in stores:
-            store.start()
-        for store in stores:
-            store.wait()
 
     if senders is None:
         fill()
@@ -68,13 +61,12 @@
         jax.ShapeDtypeStruct(((b - a) * 2 * piece + (batch if tail else 0), head), jnp.bfloat16)
         for (a, b), tail in zip(ranges, tails)
     ]
-    stages = [] if senders is None else [pltpu.VMEM(x.shape, x.dtype) for x in out_shape]
     return pl.pallas_call(
         functools.partial(pack_kernel, senders, ranges, tails),
         in_specs=[hbm] * 3,
-        out_specs=[hbm if stages else vmem] * len(ranges),
+        out_specs=[vmem] * len(ranges),
         out_shape=out_shape,
-        scratch_shapes=[pltpu.VMEM(seg.shape, jnp.int32), pltpu.SemaphoreType.DMA, pltpu.SemaphoreType.DMA] + stages,
+        scratch_shapes=[pltpu.VMEM(seg.shape, jnp.int32), pltpu.SemaphoreType.DMA, pltpu.SemaphoreType.DMA],
         compiler_params=pltpu.CompilerParams(vmem_limit_bytes=16 << 20),
         cost_estimate=pl.CostEstimate(flops=1 << 20, bytes_accessed=4 * k.size, transcendentals=0),
     )(seg, k, v)

time: 163 us -> 164 us (level)
  transfers between devices with their start and end apart: 8 -> 8, of which waited for: 3 -> 4; matrix products, arithmetic and copies ran while one was open for 0% -> 0% of each run, Pallas kernels for 16% -> 16%
where the time goes in v4:
time: 164 us; the launch traced here: 161 us
  Pallas kernels  79.6 us (49%)
  waiting for transfers between devices  66.1 us (40%)
  starting transfers between devices  10.3 us (6%)
  local copies, waits for them, and re-layouts  2.81 us (2%)
    ppermute x8, waiting for transfers between devices, shift(): return lax.ppermute(x, 'cp', pairs)  66.1 us
    pallas_call x7, Pallas kernels, attend(): pl.pallas_call(functools.partial(attend_kernel, first, last, base, size),...  47.6 us
    pallas_call x7, Pallas kernels, swap(): pl.pallas_call(swap_kernel, in_specs=[vmem], out_specs=vmem, out_shape=ja...  25 us
    ppermute x8, starting transfers between devices, shift(): return lax.ppermute(x, 'cp', pairs)  10.3 us
    pallas_call x2, Pallas kernels, pack(): pl.pallas_call(functools.partial(pack_kernel, senders, ranges, tails), in...  7.02 us
  transfers between devices with their start and end apart: 8, of which 4 were waited for; matrix products, arithmetic and copies ran while one was open for 0% of the time, Pallas kernels for 16%

profile of v4, /device:TPU:7, one launch (start us, length us, event | category | flops | bytes accessed | tf_op | source)
XLA Modules:
  0.0 161.3 jit_solution(6711521169752897842)
XLA Ops:
  0.6 6.2 %shard_map.59 = (bf16[1536,256]{1,0:T(8,128)(2,1)}, bf16[1536,256]{1,0:T(8,128)(2,1)}, bf16[1536,256]{1,0:T(8,128)(2,1)}, bf16[1024,256]{1,0:T(8,128)(2,1)S(1)},...) custom-call(s32[32,128]{1,0:T(8,128)} %seg_ref.3, ...), custom_call_target="tpu_custom_call" | custom-call | flops 1048576 | bytes 4194304 | tf_op jit(solution)/shard_map/pallas_call | solution.py:64
  6.8 1.3 collective-permute-start
  8.1 1.3 collective-permute-start.3
  9.4 1.3 collective-permute-start.2
  10.7 1.3 collective-permute-start.4
  12.0 1.3 collective-permute-start.7
  13.3 4.3 %collective-permute-done.3.mine_ref.fara_ref = bf16[768,256]{1,0:T(8,128)(2,1)S(1)} collective-permute-done((bf16[768,256]{1,0:T(8,128)(2,1)S(1)}, bf16[768,256]{1,0:T(8,128)(2,1)S(1)}, u32[]{:S(2)}, u32[]{:S(2)}) %collective-permute-start.3) | collective-permute-done | bytes 393248 | tf_op jit(solution)/shard_map/ppermute | solution.py:328
  17.6 0.0 copy-start.3
  17.6 0.7 copy-done.3
  18.3 1.3 collective-permute-start.6
  19.6 6.4 %collective-permute-done.2.mine_ref.fara_ref = bf16[768,256]{1,0:T(8,128)(2,1)S(1)} collective-permute-done((bf16[768,256]{1,0:T(8,128)(2,1)S(1)}, bf16[768,256]{1,0:T(8,128)(2,1)S(1)}, u32[]{:S(2)}, u32[]{:S(2)}) %collective-permute-start.2) | collective-permute-done | bytes 393248 | tf_op jit(solution)/shard_map/ppermute | solution.py:328
  26.0 0.0 copy-start
  26.0 1.3 collective-permute-start.5
  27.3 0.9 shard_map.60
  28.2 0.0 copy-done
  28.2 9.1 %collective-permute-done.4.mine_ref.fara_ref = bf16[1024,256]{1,0:T(8,128)(2,1)S(1)} collective-permute-done((bf16[1024,256]{1,0:T(8,128)(2,1)S(1)}, bf16[1024,256]{1,0:T(8,128)(2,1)S(1)}, u32[]{:S(2)}, u32[]{:S(2)}) %collective-permute-start.4) | collective-permute-done | bytes 524320 | tf_op jit(solution)/shard_map/ppermute | solution.py:328
  37.3 1.3 collective-permute-start.1
  38.6 0.0 copy-start.4
  38.6 1.0 copy-done.4
  39.6 8.8 %shard_map.63.farb_ref = bf16[768,256]{1,0:T(8,128)(2,1)S(1)} custom-call(bf16[768,256]{1,0:T(8,128)(2,1)S(1)} %copy-done.4), custom_call_target="tpu_custom_call" | custom-call | flops 1048576 | bytes 786432 | tf_op jit(solution)/shard_map/pallas_call | solution.py:314
  48.4 0.0 copy-start.1
  48.4 1.0 copy-done.1
  49.4 1.7 %shard_map.62.farb_ref = bf16[768,256]{1,0:T(8,128)(2,1)S(1)} custom-call(bf16[768,256]{1,0:T(8,128)(2,1)S(1)} %copy-done.1), custom_call_target="tpu_custom_call" | custom-call | flops 1048576 | bytes 786432 | tf_op jit(solution)/shard_map/pallas_call | solution.py:314
  51.1 1.9 %shard_map.64.farb_ref = bf16[1024,256]{1,0:T(8,128)(2,1)S(1)} custom-call(bf16[1024,256]{1,0:T(8,128)(2,1)S(1)} %collective-permute-done.4.mine_ref.fara_ref), custom_call_target="tpu_custom_call" | custom-call | flops 1048576 | bytes 1048576 | tf_op jit(solution)/shard_map/pallas_call | solution.py:314
  53.1 46.3 %collective-permute-done.1.mine_ref.fara_ref = bf16[1056,256]{1,0:T(8,128)(2,1)S(1)} collective-permute-done((bf16[1056,256]{1,0:T(8,128)(2,1)}, bf16[1056,256]{1,0:T(8,128)(2,1)S(1)}, u32[]{:S(2)}, u32[]{:S(2)}) %collective-permute-start.1) | collective-permute-done | bytes 540704 | tf_op jit(solution)/shard_map/ppermute | solution.py:328
  99.4 5.5 %shard_map.61.farb_ref = bf16[1056,256]{1,0:T(8,128)(2,1)S(1)} custom-call(bf16[1056,256]{1,0:T(8,128)(2,1)S(1)} %collective-permute-done.1.mine_ref.fara_ref), custom_call_target="tpu_custom_call" | custom-call | flops 1048576 | bytes 1081344 | tf_op jit(solution)/shard_map/pallas_call | solution.py:314
  104.9 0.0 collective-permute-done.7.mine_ref.fara_ref
  104.9 2.3 %shard_map.67.farb_ref = bf16[1536,256]{1,0:T(8,128)(2,1)S(1)} custom-call(bf16[1536,256]{1,0:T(8,128)(2,1)S(1)} %collective-permute-done.7.mine_ref.fara_ref), custom_call_target="tpu_custom_call" | custom-call | flops 1048576 | bytes 1572864 | tf_op jit(solution)/shard_map/pallas_call | solution.py:314
  107.3 0.0 collective-permute-done.6.mine_ref.fara_ref
  107.3 2.3 %shard_map.66.farb_ref = bf16[1536,256]{1,0:T(8,128)(2,1)S(1)} custom-call(bf16[1536,256]{1,0:T(8,128)(2,1)S(1)} %collective-permute-done.6.mine_ref.fara_ref), custom_call_target="tpu_custom_call" | custom-call | flops 1048576 | bytes 1572864 | tf_op jit(solution)/shard_map/pallas_call | solution.py:314
  109.6 0.0 collective-permute-done.5.mine_ref.fara_ref
  109.6 2.3 %shard_map.65.farb_ref = bf16[1536,256]{1,0:T(8,128)(2,1)S(1)} custom-call(bf16[1536,256]{1,0:T(8,128)(2,1)S(1)} %collective-permute-done.5.mine_ref.fara_ref), custom_call_target="tpu_custom_call" | custom-call | flops 1048576 | bytes 1572864 | tf_op jit(solution)/shard_map/pallas_call | solution.py:314
  111.9 0.0 collective-permute-done.near_ref
  111.9 0.8 subtract_reduce_fusion
  112.8 0.5 fusion.s_hbm
  113.3 0.1 broadcast_in_dim.23.cut_ref
  113.4 7.2 %shard_map.68 = (bf16[32,10,128,256]{3,2,1,0:T(8,128)(2,1)}, f32[10,32,128]{2,1,0:T(8,128)S(1)}, bf16[10,128,256]{2,1,0:T(8,128)(2,1)S(1)}, bf16[4,128,256]{2,1,0:T(8,128)(2,1)S(1)}) custom-call(s32[32]{0:T(128)} %fusion.s_hbm, s32[32,128]{1,0:T(8,128)S(1)} %broadcast_in_dim.23.cut_ref, bf16[32,10,128,256]{3,2,1,0:T(8,128)(2,1)} %bitcast.3, ...), custom_call_target="tpu_custom_call" | custom-call | flops 2684354560 | bytes 5242880 | tf_op jit(solution)/shard_map/pallas_call | solution.py:266
  120.6 8.9 %shard_map.69 = (bf16[32,10,128,256]{3,2,1,0:T(8,128)(2,1)}, f32[10,32,128]{2,1,0:T(8,128)S(1)}, bf16[10,128,256]{2,1,0:T(8,128)(2,1)S(1)}, bf16[4,128,256]{2,1,0:T(8,128)(2,1)S(1)}) custom-call(s32[32]{0:T(128)} %fusion.s_hbm, s32[32,128]{1,0:T(8,128)S(1)} %broadcast_in_dim.23.cut_ref, ...), custom_call_target="tpu_custom_call", output_to_operand_aliasing={{0}: (8, {})} | custom-call | flops 4026531840 | bytes 7864320 | tf_op jit(solution)/shard_map/pallas_call | solution.py:266
  129.5 8.0 %shard_map.70 = (bf16[32,10,128,256]{3,2,1,0:T(8,128)(2,1)}, f32[10,32,128]{2,1,0:T(8,128)S(1)}, bf16[10,128,256]{2,1,0:T(8,128)(2,1)S(1)}, bf16[4,128,256]{2,1,0:T(8,128)(2,1)S(1)}) custom-call(s32[32]{0:T(128)} %fusion.s_hbm, s32[32,128]{1,0:T(8,128)S(1)} %broadcast_in_dim.23.cut_ref, ...), custom_call_target="tpu_custom_call", output_to_operand_aliasing={{0}: (8, {})} | custom-call | flops 4026531840 | bytes 7864320 | tf_op jit(solution)/shard_map/pallas_call | solution.py:266
  137.5 8.4 %shard_map.71 = (bf16[32,10,128,256]{3,2,1,0:T(8,128)(2,1)}, f32[10,32,128]{2,1,0:T(8,128)S(1)}, bf16[10,128,256]{2,1,0:T(8,128)(2,1)S(1)}, bf16[4,128,256]{2,1,0:T(8,128)(2,1)S(1)}) custom-call(s32[32]{0:T(128)} %fusion.s_hbm, s32[32,128]{1,0:T(8,128)S(1)} %broadcast_in_dim.23.cut_ref, ...), custom_call_target="tpu_custom_call", output_to_operand_aliasing={{0}: (8, {})} | custom-call | flops 4026531840 | bytes 7864320 | tf_op jit(solution)/shard_map/pallas_call | solution.py:266
  145.9 0.0 copy-start.5
  145.9 6.2 %shard_map.72 = (bf16[32,10,128,256]{3,2,1,0:T(8,128)(2,1)}, f32[10,32,128]{2,1,0:T(8,128)S(1)}, bf16[10,128,256]{2,1,0:T(8,128)(2,1)S(1)}, bf16[4,128,256]{2,1,0:T(8,128)(2,1)S(1)}) custom-call(s32[32]{0:T(128)} %fusion.s_hbm, s32[32,128]{1,0:T(8,128)S(1)} %broadcast_in_dim.23.cut_ref, ...), custom_call_target="tpu_custom_call", output_to_operand_aliasing={{0}: (8, {})} | custom-call | flops 2684354560 | bytes 5242880 | tf_op jit(solution)/shard_map/pallas_call | solution.py:266
  152.1 0.0 copy-done.5
  152.1 0.0 copy-start.2
  152.1 4.5 %shard_map.73 = (bf16[32,10,128,256]{3,2,1,0:T(8,128)(2,1)}, f32[10,32,128]{2,1,0:T(8,128)S(1)}, bf16[10,128,256]{2,1,0:T(8,128)(2,1)S(1)}, bf16[4,128,256]{2,1,0:T(8,128)(2,1)S(1)}) custom-call(s32[32]{0:T(128)} %fusion.s_hbm, s32[32,128]{1,0:T(8,128)S(1)} %broadcast_in_dim.23.cut_ref, ...), custom_call_target="tpu_custom_call", output_to_operand_aliasing={{0}: (8, {})} | custom-call | flops 2013265920 | bytes 3932160 | tf_op jit(solution)/shard_map/pallas_call | solution.py:266
  156.6 0.0 copy-done.2
  156.6 4.5 %shard_map.74 = (bf16[32,10,128,256]{3,2,1,0:T(8,128)(2,1)}, f32[10,32,128]{2,1,0:T(8,128)}) custom-call(s32[32]{0:T(128)} %fusion.s_hbm, s32[32,128]{1,0:T(8,128)S(1)} %broadcast_in_dim.23.cut_ref, bf16[32,10,128,256]{3,2,1,0:T(8,128)(2,1)} %bitcast.9, bf16[32,128,256]{2,1,0:T(8,128)(2,1)} %k_ref.17, ...), custom_call_target="tpu_custom_call", output_to_operand_aliasing={{0}: (8, {})} | custom-call | flops 2013265920 | bytes 3932160 | tf_op jit(solution)/shard_map/pallas_call | solution.py:266
Async XLA Ops:
  6.8 105.1 %collective-permute-start = (bf16[8224,256]{1,0:T(8,128)(2,1)}, bf16[8224,256]{1,0:T(8,128)(2,1)}, u32[]{:S(2)}, u32[]{:S(2)}) collective-permute-start(bf16[8224,256]{1,0:T(8,128)(2,1)} %get-tuple-element.35), channel_id=1, source_target_pairs={{0,1},{2,3},{4,5},{6,7}} | collective-permute-start | bytes 12632072 | tf_op jit(solution)/shard_map/ppermute | solution.py:328
  8.1 9.5 %collective-permute-start.3 = (bf16[768,256]{1,0:T(8,128)(2,1)S(1)}, bf16[768,256]{1,0:T(8,128)(2,1)S(1)}, u32[]{:S(2)}, u32[]{:S(2)}) collective-permute-start(bf16[768,256]{1,0:T(8,128)(2,1)S(1)} %get-tuple-element.37), channel_id=1, source_target_pairs={{0,2},{1,3},{4,6},{5,7}} | collective-permute-start | bytes 1179656 | tf_op jit(solution)/shard_map/ppermute | solution.py:328
  9.4 16.6 %collective-permute-start.2 = (bf16[768,256]{1,0:T(8,128)(2,1)S(1)}, bf16[768,256]{1,0:T(8,128)(2,1)S(1)}, u32[]{:S(2)}, u32[]{:S(2)}) collective-permute-start(bf16[768,256]{1,0:T(8,128)(2,1)S(1)} %get-tuple-element.36), channel_id=1, source_target_pairs={{0,2},{1,3},{4,6},{5,7}} | collective-permute-start | bytes 1179656 | tf_op jit(solution)/shard_map/ppermute | solution.py:328
  10.7 26.6 %collective-permute-start.4 = (bf16[1024,256]{1,0:T(8,128)(2,1)S(1)}, bf16[1024,256]{1,0:T(8,128)(2,1)S(1)}, u32[]{:S(2)}, u32[]{:S(2)}) collective-permute-start(bf16[1024,256]{1,0:T(8,128)(2,1)S(1)} %get-tuple-element.38), channel_id=1, source_target_pairs={{0,2},{1,3},{4,6},{5,7}} | collective-permute-start | bytes 1572872 | tf_op jit(solution)/shard_map/ppermute | solution.py:328
  12.0 92.9 %collective-permute-start.7 = (bf16[1536,256]{1,0:T(8,128)(2,1)}, bf16[1536,256]{1,0:T(8,128)(2,1)S(1)}, u32[]{:S(2)}, u32[]{:S(2)}) collective-permute-start(bf16[1536,256]{1,0:T(8,128)(2,1)} %get-tuple-element.41), channel_id=1, source_target_pairs={{0,2},{1,3},{4,6},{5,7}} | collective-permute-start | bytes 2359304 | tf_op jit(solution)/shard_map/ppermute | solution.py:328
  17.6 0.7 copy-start.3
  18.3 88.9 %collective-permute-start.6 = (bf16[1536,256]{1,0:T(8,128)(2,1)}, bf16[1536,256]{1,0:T(8,128)(2,1)S(1)}, u32[]{:S(2)}, u32[]{:S(2)}) collective-permute-start(bf16[1536,256]{1,0:T(8,128)(2,1)} %get-tuple-element.40), channel_id=1, source_target_pairs={{0,2},{1,3},{4,6},{5,7}} | collective-permute-start | bytes 2359304 | tf_op jit(solution)/shard_map/ppermute | solution.py:328
  26.0 2.2 %copy-start = (bf16[768,256]{1,0:T(8,128)(2,1)}, bf16[768,256]{1,0:T(8,128)(2,1)S(1)}, u32[]{:S(2)}) copy-start(bf16[768,256]{1,0:T(8,128)(2,1)S(1)} %collective-permute-done.2.mine_ref.fara_ref) | copy-start | bytes 1179652
  26.0 83.6 %collective-permute-start.5 = (bf16[1536,256]{1,0:T(8,128)(2,1)}, bf16[1536,256]{1,0:T(8,128)(2,1)S(1)}, u32[]{:S(2)}, u32[]{:S(2)}) collective-permute-start(bf16[1536,256]{1,0:T(8,128)(2,1)} %get-tuple-element.39), channel_id=1, source_target_pairs={{0,2},{1,3},{4,6},{5,7}} | collective-permute-start | bytes 2359304 | tf_op jit(solution)/shard_map/ppermute | solution.py:328
  37.3 62.1 %collective-permute-start.1 = (bf16[1056,256]{1,0:T(8,128)(2,1)}, bf16[1056,256]{1,0:T(8,128)(2,1)S(1)}, u32[]{:S(2)}, u32[]{:S(2)}) collective-permute-start(bf16[1056,256]{1,0:T(8,128)(2,1)} %shard_map.60), channel_id=1, source_target_pairs={{0,2},{1,3},{4,6},{5,7}} | collective-permute-start | bytes 1622024 | tf_op jit(solution)/shard_map/ppermute | solution.py:328
  38.6 1.0 copy-start.4
  48.4 1.0 copy-start.1
  145.9 6.2 %copy-start.5 = (bf16[768,256]{1,0:T(8,128)(2,1)S(1)}, bf16[768,256]{1,0:T(8,128)(2,1)}, u32[]{:S(2)}) copy-start(bf16[768,256]{1,0:T(8,128)(2,1)} %copy-done.3) | copy-start | bytes 1179652
  152.1 4.5 %copy-start.2 = (bf16[768,256]{1,0:T(8,128)(2,1)S(1)}, bf16[768,256]{1,0:T(8,128)(2,1)}, u32[]{:S(2)}) copy-start(bf16[768,256]{1,0:T(8,128)(2,1)} %copy-done) | copy-start | bytes 1179652

commit v5 on v4

--- a/solution.py
+++ b/solution.py
@@ -176,10 +176,12 @@
         logs = finish(groups - 1, logs, *before)
         lse_ref[:, pl.ds(seq, 1), :] = logs.T[:heads][:, None, :]
 
-    n_ref[0] = jnp.where(me >= 2, 4, 2)
+    n_ref[0] = jnp.maximum(me + 1, 2)
     if first:
         load(0)
     else:
+        for step in range(1, min(3, size)):
+            load(step)
         q_buf[0] = q_in[...]
         there = pl.ds(pl.multiple_of(jnp.where(odd == 1, 1, 3) * piece, piece), piece)
         for half, buf in enumerate((k_buf, v_buf)):
@@ -196,11 +198,12 @@
             for g in range(groups):
                 q_load(step, g).wait()
 
-        @pl.when((step == 0) & (size > 1))
-        def _():
-            load(1)
-
-        @pl.when(step + 2 < size)
+        @pl.when((step == 0) & first)
+        def _():
+            for at in range(1, min(3, size)):
+                load(at)
+
+        @pl.when((step > 0) & (step + 2 < size))
         def _():
             load(step + 2)
 

time: 164 us -> 164 us (level)
  no operation moved by 1% of the time
where the time goes in v5:
time: 164 us; the launch traced here: 161 us
  Pallas kernels  79.7 us (49%)
  waiting for transfers between devices  66.1 us (40%)
  starting transfers between devices  10.3 us (6%)
  local copies, waits for them, and re-layouts  2.81 us (2%)
    ppermute x8, waiting for transfers between devices, shift(): return lax.ppermute(x, 'cp', pairs)  66.1 us
    pallas_call x7, Pallas kernels, attend(): pl.pallas_call(functools.partial(attend_kernel, first, last, base, size),...  47.7 us
    pallas_call x7, Pallas kernels, swap(): pl.pallas_call(swap_kernel, in_specs=[vmem], out_specs=vmem, out_shape=ja...  25 us
    ppermute x8, starting transfers between devices, shift(): return lax.ppermute(x, 'cp', pairs)  10.3 us
    pallas_call x2, Pallas kernels, pack(): pl.pallas_call(functools.partial(pack_kernel, senders, ranges, tails), in...  7.02 us
  transfers between devices with their start and end apart: 8, of which 4 were waited for; matrix products, arithmetic and copies ran while one was open for 0% of the time, Pallas kernels for 16%

profile of v5, /device:TPU:7, one launch (start us, length us, event | category | flops | bytes accessed | tf_op | source)
XLA Modules:
  0.0 161.4 jit_solution(14119513836076063462)
XLA Ops:
  0.6 6.2 %shard_map.59 = (bf16[1536,256]{1,0:T(8,128)(2,1)}, bf16[1536,256]{1,0:T(8,128)(2,1)}, bf16[1536,256]{1,0:T(8,128)(2,1)}, bf16[1024,256]{1,0:T(8,128)(2,1)S(1)},...) custom-call(s32[32,128]{1,0:T(8,128)} %seg_ref.3, ...), custom_call_target="tpu_custom_call" | custom-call | flops 1048576 | bytes 4194304 | tf_op jit(solution)/shard_map/pallas_call | solution.py:64
  6.8 1.3 collective-permute-start
  8.1 1.3 collective-permute-start.3
  9.4 1.3 collective-permute-start.2
  10.7 1.3 collective-permute-start.4
  12.0 1.3 collective-permute-start.7
  13.3 4.3 %collective-permute-done.3.mine_ref.fara_ref = bf16[768,256]{1,0:T(8,128)(2,1)S(1)} collective-permute-done((bf16[768,256]{1,0:T(8,128)(2,1)S(1)}, bf16[768,256]{1,0:T(8,128)(2,1)S(1)}, u32[]{:S(2)}, u32[]{:S(2)}) %collective-permute-start.3) | collective-permute-done | bytes 393248 | tf_op jit(solution)/shard_map/ppermute | solution.py:331
  17.6 0.0 copy-start.3
  17.6 0.7 copy-done.3
  18.3 1.3 collective-permute-start.6
  19.6 6.4 %collective-permute-done.2.mine_ref.fara_ref = bf16[768,256]{1,0:T(8,128)(2,1)S(1)} collective-permute-done((bf16[768,256]{1,0:T(8,128)(2,1)S(1)}, bf16[768,256]{1,0:T(8,128)(2,1)S(1)}, u32[]{:S(2)}, u32[]{:S(2)}) %collective-permute-start.2) | collective-permute-done | bytes 393248 | tf_op jit(solution)/shard_map/ppermute | solution.py:331
  26.0 0.0 copy-start
  26.0 1.3 collective-permute-start.5
  27.3 0.9 shard_map.60
  28.2 0.0 copy-done
  28.2 9.1 %collective-permute-done.4.mine_ref.fara_ref = bf16[1024,256]{1,0:T(8,128)(2,1)S(1)} collective-permute-done((bf16[1024,256]{1,0:T(8,128)(2,1)S(1)}, bf16[1024,256]{1,0:T(8,128)(2,1)S(1)}, u32[]{:S(2)}, u32[]{:S(2)}) %collective-permute-start.4) | collective-permute-done | bytes 524320 | tf_op jit(solution)/shard_map/ppermute | solution.py:331
  37.3 1.3 collective-permute-start.1
  38.6 0.0 copy-start.4
  38.6 1.0 copy-done.4
  39.6 8.8 %shard_map.63.farb_ref = bf16[768,256]{1,0:T(8,128)(2,1)S(1)} custom-call(bf16[768,256]{1,0:T(8,128)(2,1)S(1)} %copy-done.4), custom_call_target="tpu_custom_call" | custom-call | flops 1048576 | bytes 786432 | tf_op jit(solution)/shard_map/pallas_call | solution.py:317
  48.4 0.0 copy-start.1
  48.4 1.0 copy-done.1
  49.4 1.7 %shard_map.62.farb_ref = bf16[768,256]{1,0:T(8,128)(2,1)S(1)} custom-call(bf16[768,256]{1,0:T(8,128)(2,1)S(1)} %copy-done.1), custom_call_target="tpu_custom_call" | custom-call | flops 1048576 | bytes 786432 | tf_op jit(solution)/shard_map/pallas_call | solution.py:317
  51.1 1.9 %shard_map.64.farb_ref = bf16[1024,256]{1,0:T(8,128)(2,1)S(1)} custom-call(bf16[1024,256]{1,0:T(8,128)(2,1)S(1)} %collective-permute-done.4.mine_ref.fara_ref), custom_call_target="tpu_custom_call" | custom-call | flops 1048576 | bytes 1048576 | tf_op jit(solution)/shard_map/pallas_call | solution.py:317
  53.1 46.3 %collective-permute-done.1.mine_ref.fara_ref = bf16[1056,256]{1,0:T(8,128)(2,1)S(1)} collective-permute-done((bf16[1056,256]{1,0:T(8,128)(2,1)}, bf16[1056,256]{1,0:T(8,128)(2,1)S(1)}, u32[]{:S(2)}, u32[]{:S(2)}) %collective-permute-start.1) | collective-permute-done | bytes 540704 | tf_op jit(solution)/shard_map/ppermute | solution.py:331
  99.4 5.5 %shard_map.61.farb_ref = bf16[1056,256]{1,0:T(8,128)(2,1)S(1)} custom-call(bf16[1056,256]{1,0:T(8,128)(2,1)S(1)} %collective-permute-done.1.mine_ref.fara_ref), custom_call_target="tpu_custom_call" | custom-call | flops 1048576 | bytes 1081344 | tf_op jit(solution)/shard_map/pallas_call | solution.py:317
  104.9 0.0 collective-permute-done.7.mine_ref.fara_ref
  104.9 2.3 %shard_map.67.farb_ref = bf16[1536,256]{1,0:T(8,128)(2,1)S(1)} custom-call(bf16[1536,256]{1,0:T(8,128)(2,1)S(1)} %collective-permute-done.7.mine_ref.fara_ref), custom_call_target="tpu_custom_call" | custom-call | flops 1048576 | bytes 1572864 | tf_op jit(solution)/shard_map/pallas_call | solution.py:317
  107.3 0.0 collective-permute-done.6.mine_ref.fara_ref
  107.3 2.3 %shard_map.66.farb_ref = bf16[1536,256]{1,0:T(8,128)(2,1)S(1)} custom-call(bf16[1536,256]{1,0:T(8,128)(2,1)S(1)} %collective-permute-done.6.mine_ref.fara_ref), custom_call_target="tpu_custom_call" | custom-call | flops 1048576 | bytes 1572864 | tf_op jit(solution)/shard_map/pallas_call | solution.py:317
  109.6 0.0 collective-permute-done.5.mine_ref.fara_ref
  109.6 2.3 %shard_map.65.farb_ref = bf16[1536,256]{1,0:T(8,128)(2,1)S(1)} custom-call(bf16[1536,256]{1,0:T(8,128)(2,1)S(1)} %collective-permute-done.5.mine_ref.fara_ref), custom_call_target="tpu_custom_call" | custom-call | flops 1048576 | bytes 1572864 | tf_op jit(solution)/shard_map/pallas_call | solution.py:317
  111.9 0.0 collective-permute-done.near_ref
  111.9 0.8 subtract_reduce_fusion
  112.8 0.5 fusion.s_hbm
  113.3 0.1 broadcast_in_dim.23.cut_ref
  113.4 7.2 %shard_map.68 = (bf16[32,10,128,256]{3,2,1,0:T(8,128)(2,1)}, f32[10,32,128]{2,1,0:T(8,128)S(1)}, bf16[10,128,256]{2,1,0:T(8,128)(2,1)S(1)}, bf16[4,128,256]{2,1,0:T(8,128)(2,1)S(1)}) custom-call(s32[32]{0:T(128)} %fusion.s_hbm, s32[32,128]{1,0:T(8,128)S(1)} %broadcast_in_dim.23.cut_ref, bf16[32,10,128,256]{3,2,1,0:T(8,128)(2,1)} %bitcast.3, ...), custom_call_target="tpu_custom_call" | custom-call | flops 2684354560 | bytes 5242880 | tf_op jit(solution)/shard_map/pallas_call | solution.py:269
  120.6 8.9 %shard_map.69 = (bf16[32,10,128,256]{3,2,1,0:T(8,128)(2,1)}, f32[10,32,128]{2,1,0:T(8,128)S(1)}, bf16[10,128,256]{2,1,0:T(8,128)(2,1)S(1)}, bf16[4,128,256]{2,1,0:T(8,128)(2,1)S(1)}) custom-call(s32[32]{0:T(128)} %fusion.s_hbm, s32[32,128]{1,0:T(8,128)S(1)} %broadcast_in_dim.23.cut_ref, ...), custom_call_target="tpu_custom_call", output_to_operand_aliasing={{0}: (8, {})} | custom-call | flops 4026531840 | bytes 7864320 | tf_op jit(solution)/shard_map/pallas_call | solution.py:269
  129.5 8.0 %shard_map.70 = (bf16[32,10,128,256]{3,2,1,0:T(8,128)(2,1)}, f32[10,32,128]{2,1,0:T(8,128)S(1)}, bf16[10,128,256]{2,1,0:T(8,128)(2,1)S(1)}, bf16[4,128,256]{2,1,0:T(8,128)(2,1)S(1)}) custom-call(s32[32]{0:T(128)} %fusion.s_hbm, s32[32,128]{1,0:T(8,128)S(1)} %broadcast_in_dim.23.cut_ref, ...), custom_call_target="tpu_custom_call", output_to_operand_aliasing={{0}: (8, {})} | custom-call | flops 4026531840 | bytes 7864320 | tf_op jit(solution)/shard_map/pallas_call | solution.py:269
  137.5 8.4 %shard_map.71 = (bf16[32,10,128,256]{3,2,1,0:T(8,128)(2,1)}, f32[10,32,128]{2,1,0:T(8,128)S(1)}, bf16[10,128,256]{2,1,0:T(8,128)(2,1)S(1)}, bf16[4,128,256]{2,1,0:T(8,128)(2,1)S(1)}) custom-call(s32[32]{0:T(128)} %fusion.s_hbm, s32[32,128]{1,0:T(8,128)S(1)} %broadcast_in_dim.23.cut_ref, ...), custom_call_target="tpu_custom_call", output_to_operand_aliasing={{0}: (8, {})} | custom-call | flops 4026531840 | bytes 7864320 | tf_op jit(solution)/shard_map/pallas_call | solution.py:269
  146.0 0.0 copy-start.5
  146.0 6.2 %shard_map.72 = (bf16[32,10,128,256]{3,2,1,0:T(8,128)(2,1)}, f32[10,32,128]{2,1,0:T(8,128)S(1)}, bf16[10,128,256]{2,1,0:T(8,128)(2,1)S(1)}, bf16[4,128,256]{2,1,0:T(8,128)(2,1)S(1)}) custom-call(s32[32]{0:T(128)} %fusion.s_hbm, s32[32,128]{1,0:T(8,128)S(1)} %broadcast_in_dim.23.cut_ref, ...), custom_call_target="tpu_custom_call", output_to_operand_aliasing={{0}: (8, {})} | custom-call | flops 2684354560 | bytes 5242880 | tf_op jit(solution)/shard_map/pallas_call | solution.py:269
  152.1 0.0 copy-done.5
  152.2 0.0 copy-start.2
  152.2 4.5 %shard_map.73 = (bf16[32,10,128,256]{3,2,1,0:T(8,128)(2,1)}, f32[10,32,128]{2,1,0:T(8,128)S(1)}, bf16[10,128,256]{2,1,0:T(8,128)(2,1)S(1)}, bf16[4,128,256]{2,1,0:T(8,128)(2,1)S(1)}) custom-call(s32[32]{0:T(128)} %fusion.s_hbm, s32[32,128]{1,0:T(8,128)S(1)} %broadcast_in_dim.23.cut_ref, ...), custom_call_target="tpu_custom_call", output_to_operand_aliasing={{0}: (8, {})} | custom-call | flops 2013265920 | bytes 3932160 | tf_op jit(solution)/shard_map/pallas_call | solution.py:269
  156.7 0.0 copy-done.2
  156.7 4.5 %shard_map.74 = (bf16[32,10,128,256]{3,2,1,0:T(8,128)(2,1)}, f32[10,32,128]{2,1,0:T(8,128)}) custom-call(s32[32]{0:T(128)} %fusion.s_hbm, s32[32,128]{1,0:T(8,128)S(1)} %broadcast_in_dim.23.cut_ref, bf16[32,10,128,256]{3,2,1,0:T(8,128)(2,1)} %bitcast.9, bf16[32,128,256]{2,1,0:T(8,128)(2,1)} %k_ref.17, ...), custom_call_target="tpu_custom_call", output_to_operand_aliasing={{0}: (8, {})} | custom-call | flops 2013265920 | bytes 3932160 | tf_op jit(solution)/shard_map/pallas_call | solution.py:269
Async XLA Ops:
  6.8 105.1 %collective-permute-start = (bf16[8224,256]{1,0:T(8,128)(2,1)}, bf16[8224,256]{1,0:T(8,128)(2,1)}, u32[]{:S(2)}, u32[]{:S(2)}) collective-permute-start(bf16[8224,256]{1,0:T(8,128)(2,1)} %get-tuple-element.35), channel_id=1, source_target_pairs={{0,1},{2,3},{4,5},{6,7}} | collective-permute-start | bytes 12632072 | tf_op jit(solution)/shard_map/ppermute | solution.py:331
  8.1 9.5 %collective-permute-start.3 = (bf16[768,256]{1,0:T(8,128)(2,1)S(1)}, bf16[768,256]{1,0:T(8,128)(2,1)S(1)}, u32[]{:S(2)}, u32[]{:S(2)}) collective-permute-start(bf16[768,256]{1,0:T(8,128)(2,1)S(1)} %get-tuple-element.37), channel_id=1, source_target_pairs={{0,2},{1,3},{4,6},{5,7}} | collective-permute-start | bytes 1179656 | tf_op jit(solution)/shard_map/ppermute | solution.py:331
  9.4 16.6 %collective-permute-start.2 = (bf16[768,256]{1,0:T(8,128)(2,1)S(1)}, bf16[768,256]{1,0:T(8,128)(2,1)S(1)}, u32[]{:S(2)}, u32[]{:S(2)}) collective-permute-start(bf16[768,256]{1,0:T(8,128)(2,1)S(1)} %get-tuple-element.36), channel_id=1, source_target_pairs={{0,2},{1,3},{4,6},{5,7}} | collective-permute-start | bytes 1179656 | tf_op jit(solution)/shard_map/ppermute | solution.py:331
  10.7 26.6 %collective-permute-start.4 = (bf16[1024,256]{1,0:T(8,128)(2,1)S(1)}, bf16[1024,256]{1,0:T(8,128)(2,1)S(1)}, u32[]{:S(2)}, u32[]{:S(2)}) collective-permute-start(bf16[1024,256]{1,0:T(8,128)(2,1)S(1)} %get-tuple-element.38), channel_id=1, source_target_pairs={{0,2},{1,3},{4,6},{5,7}} | collective-permute-start | bytes 1572872 | tf_op jit(solution)/shard_map/ppermute | solution.py:331
  12.0 92.9 %collective-permute-start.7 = (bf16[1536,256]{1,0:T(8,128)(2,1)}, bf16[1536,256]{1,0:T(8,128)(2,1)S(1)}, u32[]{:S(2)}, u32[]{:S(2)}) collective-permute-start(bf16[1536,256]{1,0:T(8,128)(2,1)} %get-tuple-element.41), channel_id=1, source_target_pairs={{0,2},{1,3},{4,6},{5,7}} | collective-permute-start | bytes 2359304 | tf_op jit(solution)/shard_map/ppermute | solution.py:331
  17.6 0.7 copy-start.3
  18.3 88.9 %collective-permute-start.6 = (bf16[1536,256]{1,0:T(8,128)(2,1)}, bf16[1536,256]{1,0:T(8,128)(2,1)S(1)}, u32[]{:S(2)}, u32[]{:S(2)}) collective-permute-start(bf16[1536,256]{1,0:T(8,128)(2,1)} %get-tuple-element.40), channel_id=1, source_target_pairs={{0,2},{1,3},{4,6},{5,7}} | collective-permute-start | bytes 2359304 | tf_op jit(solution)/shard_map/ppermute | solution.py:331
  26.0 2.2 %copy-start = (bf16[768,256]{1,0:T(8,128)(2,1)}, bf16[768,256]{1,0:T(8,128)(2,1)S(1)}, u32[]{:S(2)}) copy-start(bf16[768,256]{1,0:T(8,128)(2,1)S(1)} %collective-permute-done.2.mine_ref.fara_ref) | copy-start | bytes 1179652
  26.0 83.6 %collective-permute-start.5 = (bf16[1536,256]{1,0:T(8,128)(2,1)}, bf16[1536,256]{1,0:T(8,128)(2,1)S(1)}, u32[]{:S(2)}, u32[]{:S(2)}) collective-permute-start(bf16[1536,256]{1,0:T(8,128)(2,1)} %get-tuple-element.39), channel_id=1, source_target_pairs={{0,2},{1,3},{4,6},{5,7}} | collective-permute-start | bytes 2359304 | tf_op jit(solution)/shard_map/ppermute | solution.py:331
  37.3 62.1 %collective-permute-start.1 = (bf16[1056,256]{1,0:T(8,128)(2,1)}, bf16[1056,256]{1,0:T(8,128)(2,1)S(1)}, u32[]{:S(2)}, u32[]{:S(2)}) collective-permute-start(bf16[1056,256]{1,0:T(8,128)(2,1)} %shard_map.60), channel_id=1, source_target_pairs={{0,2},{1,3},{4,6},{5,7}} | collective-permute-start | bytes 1622024 | tf_op jit(solution)/shard_map/ppermute | solution.py:331
  38.6 1.0 copy-start.4
  48.4 1.0 copy-start.1
  146.0 6.2 %copy-start.5 = (bf16[768,256]{1,0:T(8,128)(2,1)S(1)}, bf16[768,256]{1,0:T(8,128)(2,1)}, u32[]{:S(2)}) copy-start(bf16[768,256]{1,0:T(8,128)(2,1)} %copy-done.3) | copy-start | bytes 1179652
  152.2 4.5 %copy-start.2 = (bf16[768,256]{1,0:T(8,128)(2,1)S(1)}, bf16[768,256]{1,0:T(8,128)(2,1)}, u32[]{:S(2)}) copy-start(bf16[768,256]{1,0:T(8,128)(2,1)} %copy-done) | copy-start | bytes 1179652

commit v6 on v5

--- a/solution.py
+++ b/solution.py
@@ -8,7 +8,7 @@
 from jax.sharding import PartitionSpec as P
 
 
-CHUNKS = (4, 6, 6, 6, 4, 3, 3)
+CHUNKS = (4, 6, 6, 7, 4, 3, 2)
 BOUNDS = tuple(sum(CHUNKS[:n]) for n in range(len(CHUNKS) + 1))
 GROUP = 2
 DEPTH = 3
@@ -37,7 +37,9 @@
                     copy.start()
         segments.wait()
         here = jnp.sum((seg_scr[...] == 0).astype(jnp.float32), axis=1, keepdims=True)
-        rows = jnp.broadcast_to(here, (batch, head)).astype(jnp.bfloat16)
+        half = (batch // 2, head // 2)
+        rows = [jnp.broadcast_to(x, half) for x in (here[:half[0]], here[half[0]:])]
+        rows = jnp.concatenate(rows, axis=1).astype(jnp.bfloat16)
         for out, (a, b), tail in zip(outs, ranges, tails):
             if tail:
                 out[(b - a) * 2 * piece:] = rows
@@ -58,7 +60,7 @@
     vmem, hbm = pl.BlockSpec(memory_space=pltpu.VMEM), pl.BlockSpec(memory_space=pltpu.HBM)
     seg, k, v = (pltpu.with_memory_space_constraint(x, pltpu.HBM) for x in (seg, k, v))
     out_shape = [
-        jax.ShapeDtypeStruct(((b - a) * 2 * piece + (batch if tail else 0), head), jnp.bfloat16)
+        jax.ShapeDtypeStruct(((b - a) * 2 * piece + (batch // 2 if tail else 0), head), jnp.bfloat16)
         for (a, b), tail in zip(ranges, tails)
     ]
     return pl.pallas_call(
@@ -333,7 +335,7 @@
 
 def solution(mesh):
     def local(q_loc, k_loc, v_loc, seg_loc):
-        batch, piece, _, _ = q_loc.shape
+        batch, piece, _, head = q_loc.shape
         me = lax.axis_index("cp")
         q = jnp.transpose(q_loc, (0, 2, 1, 3))
         ranges = tuple(zip(BOUNDS[:-1], BOUNDS[1:]))
@@ -345,7 +347,8 @@
         farb = [swap(n, x) for n, x in enumerate(fara)]
 
         def zeros(packed, there):
-            return jnp.where(there, packed[-batch:, 0].astype(jnp.int32), 0)
+            halves = jnp.concatenate([packed[-batch // 2:, at] for at in (0, head // 2)])
+            return jnp.where(there, halves.astype(jnp.int32), 0)
 
         odd, upper = me % 2 == 1, me >= 2
         cuts = zeros(whole, True) + zeros(near, odd) + zeros(fara[0], upper) + zeros(farb[0], upper)

time: 164 us -> 163 us (level)
  local copies, waits for them, and re-layouts: 2.81 us -> 4.46 us
    slice x0 -> x3, local copies, waits for them, and re-layouts: none -> 1.74 us  [zeros(): packed[-batch // 2:, at]]
  transfers between devices with their start and end apart: 8 -> 8, of which waited for: 4 -> 2; matrix products, arithmetic and copies ran while one was open for 0% -> 1% of each run, Pallas kernels for 16% -> 16%
where the time goes in v6:
time: 163 us; the launch traced here: 162 us
  Pallas kernels  79.6 us (49%)
  waiting for transfers between devices  65.4 us (40%)
  starting transfers between devices  10.3 us (6%)
  local copies, waits for them, and re-layouts  4.46 us (3%)
    ppermute x8, waiting for transfers between devices, shift(): return lax.ppermute(x, 'cp', pairs)  65.4 us
    pallas_call x7, Pallas kernels, attend(): pl.pallas_call(functools.partial(attend_kernel, first, last, base, size),...  47.7 us
    pallas_call x7, Pallas kernels, swap(): pl.pallas_call(swap_kernel, in_specs=[vmem], out_specs=vmem, out_shape=ja...  24.9 us
    ppermute x8, starting transfers between devices, shift(): return lax.ppermute(x, 'cp', pairs)  10.3 us
    pallas_call x2, Pallas kernels, pack(): pl.pallas_call(functools.partial(pack_kernel, senders, ranges, tails), in...  7.02 us
  transfers between devices with their start and end apart: 8, of which 2 were waited for; matrix products, arithmetic and copies ran while one was open for 1% of the time, Pallas kernels for 16%

profile of v6, /device:TPU:7, one launch (start us, length us, event | category | flops | bytes accessed | tf_op | source)
XLA Modules:
  0.0 161.5 jit_solution(16824848504114722733)
XLA Ops:
  0.6 6.2 %shard_map.59 = (bf16[1536,256]{1,0:T(8,128)(2,1)}, bf16[1536,256]{1,0:T(8,128)(2,1)}, bf16[1792,256]{1,0:T(8,128)(2,1)}, bf16[1024,256]{1,0:T(8,128)(2,1)S(1)},...) custom-call(s32[32,128]{1,0:T(8,128)} %seg_ref.3, ...), custom_call_target="tpu_custom_call" | custom-call | flops 1048576 | bytes 4194304 | tf_op jit(solution)/shard_map/pallas_call | solution.py:66
  6.8 1.3 collective-permute-start
  8.1 1.3 collective-permute-start.3
  9.4 1.3 collective-permute-start.4
  10.7 1.3 collective-permute-start.2
  12.0 1.3 collective-permute-start.5
  13.3 21.2 %collective-permute-done.2.mine_ref.fara_ref = bf16[512,256]{1,0:T(8,128)(2,1)S(1)} collective-permute-done((bf16[512,256]{1,0:T(8,128)(2,1)S(1)}, bf16[512,256]{1,0:T(8,128)(2,1)S(1)}, u32[]{:S(2)}, u32[]{:S(2)}) %collective-permute-start.2) | collective-permute-done | bytes 262176 | tf_op jit(solution)/shard_map/ppermute | solution.py:333
  34.5 0.7 copy-done.3
  35.2 1.3 collective-permute-start.7
  36.5 0.0 collective-permute-done.3.mine_ref.fara_ref
  36.5 0.0 copy-start
  36.5 1.3 collective-permute-start.6
  37.8 0.8 shard_map.60
  38.6 0.0 copy-done
  38.6 0.0 collective-permute-done.4.mine_ref.fara_ref
  38.7 1.3 collective-permute-start.1
  40.0 0.8 slice_reduce_fusion.7
  40.8 1.0 copy-done.4
  41.7 8.6 %shard_map.62.farb_ref = bf16[512,256]{1,0:T(8,128)(2,1)S(1)} custom-call(bf16[512,256]{1,0:T(8,128)(2,1)S(1)} %copy-done.4), custom_call_target="tpu_custom_call" | custom-call | flops 1048576 | bytes 524288 | tf_op jit(solution)/shard_map/pallas_call | solution.py:319
  50.4 0.0 copy-start.1
  50.4 1.0 copy-done.1
  51.4 1.7 %shard_map.63.farb_ref = bf16[768,256]{1,0:T(8,128)(2,1)S(1)} custom-call(bf16[768,256]{1,0:T(8,128)(2,1)S(1)} %copy-done.1), custom_call_target="tpu_custom_call" | custom-call | flops 1048576 | bytes 786432 | tf_op jit(solution)/shard_map/pallas_call | solution.py:319
  53.1 1.9 %shard_map.64.farb_ref = bf16[1024,256]{1,0:T(8,128)(2,1)S(1)} custom-call(bf16[1024,256]{1,0:T(8,128)(2,1)S(1)} %collective-permute-done.4.mine_ref.fara_ref), custom_call_target="tpu_custom_call" | custom-call | flops 1048576 | bytes 1048576 | tf_op jit(solution)/shard_map/pallas_call | solution.py:319
  55.1 44.2 %collective-permute-done.1.mine_ref.fara_ref = bf16[1040,256]{1,0:T(8,128)(2,1)S(1)} collective-permute-done((bf16[1040,256]{1,0:T(8,128)(2,1)}, bf16[1040,256]{1,0:T(8,128)(2,1)S(1)}, u32[]{:S(2)}, u32[]{:S(2)}) %collective-permute-start.1) | collective-permute-done | bytes 532512 | tf_op jit(solution)/shard_map/ppermute | solution.py:333
  99.3 5.5 %shard_map.61.farb_ref = bf16[1040,256]{1,0:T(8,128)(2,1)S(1)} custom-call(bf16[1040,256]{1,0:T(8,128)(2,1)S(1)} %collective-permute-done.1.mine_ref.fara_ref), custom_call_target="tpu_custom_call" | custom-call | flops 1048576 | bytes 1064960 | tf_op jit(solution)/shard_map/pallas_call | solution.py:319
  104.8 0.1 slice_reduce_fusion.1
  104.9 0.0 collective-permute-done.7.mine_ref.fara_ref
  104.9 2.3 %shard_map.67.farb_ref = bf16[1536,256]{1,0:T(8,128)(2,1)S(1)} custom-call(bf16[1536,256]{1,0:T(8,128)(2,1)S(1)} %collective-permute-done.7.mine_ref.fara_ref), custom_call_target="tpu_custom_call" | custom-call | flops 1048576 | bytes 1572864 | tf_op jit(solution)/shard_map/pallas_call | solution.py:319
  107.2 0.0 collective-permute-done.6.mine_ref.fara_ref
  107.2 2.3 %shard_map.66.farb_ref = bf16[1536,256]{1,0:T(8,128)(2,1)S(1)} custom-call(bf16[1536,256]{1,0:T(8,128)(2,1)S(1)} %collective-permute-done.6.mine_ref.fara_ref), custom_call_target="tpu_custom_call" | custom-call | flops 1048576 | bytes 1572864 | tf_op jit(solution)/shard_map/pallas_call | solution.py:319
  109.6 0.0 collective-permute-done.5.mine_ref.fara_ref
  109.6 2.5 %shard_map.65.farb_ref = bf16[1792,256]{1,0:T(8,128)(2,1)S(1)} custom-call(bf16[1792,256]{1,0:T(8,128)(2,1)S(1)} %collective-permute-done.5.mine_ref.fara_ref), custom_call_target="tpu_custom_call" | custom-call | flops 1048576 | bytes 1835008 | tf_op jit(solution)/shard_map/pallas_call | solution.py:319
  112.1 0.0 collective-permute-done.near_ref
  112.1 0.8 slice_reduce_fusion.3
  112.9 0.1 broadcast_subtract_fusion
  113.0 0.6 fusion.3.s_hbm
  113.5 0.1 broadcast_in_dim.17.cut_ref
  113.6 7.2 %shard_map.68 = (bf16[32,10,128,256]{3,2,1,0:T(8,128)(2,1)}, f32[10,32,128]{2,1,0:T(8,128)S(1)}, bf16[10,128,256]{2,1,0:T(8,128)(2,1)S(1)}, bf16[4,128,256]{2,1,0:T(8,128)(2,1)S(1)}) custom-call(s32[32]{0:T(128)} %fusion.3.s_hbm, s32[32,128]{1,0:T(8,128)S(1)} %broadcast_in_dim.17.cut_ref, bf16[32,10,128,256]{3,2,1,0:T(8,128)(2,1)} %bitcast.3, ...), custom_call_target="tpu_custom_call" | custom-call | flops 2684354560 | bytes 5242880 | tf_op jit(solution)/shard_map/pallas_call | solution.py:271
  120.8 8.9 %shard_map.69 = (bf16[32,10,128,256]{3,2,1,0:T(8,128)(2,1)}, f32[10,32,128]{2,1,0:T(8,128)S(1)}, bf16[10,128,256]{2,1,0:T(8,128)(2,1)S(1)}, bf16[4,128,256]{2,1,0:T(8,128)(2,1)S(1)}) custom-call(s32[32]{0:T(128)} %fusion.3.s_hbm, s32[32,128]{1,0:T(8,128)S(1)} %broadcast_in_dim.17.cut_ref, ...), custom_call_target="tpu_custom_call", output_to_operand_aliasing={{0}: (8, {})} | custom-call | flops 4026531840 | bytes 7864320 | tf_op jit(solution)/shard_map/pallas_call | solution.py:271
  129.7 8.0 %shard_map.70 = (bf16[32,10,128,256]{3,2,1,0:T(8,128)(2,1)}, f32[10,32,128]{2,1,0:T(8,128)S(1)}, bf16[10,128,256]{2,1,0:T(8,128)(2,1)S(1)}, bf16[4,128,256]{2,1,0:T(8,128)(2,1)S(1)}) custom-call(s32[32]{0:T(128)} %fusion.3.s_hbm, s32[32,128]{1,0:T(8,128)S(1)} %broadcast_in_dim.17.cut_ref, ...), custom_call_target="tpu_custom_call", output_to_operand_aliasing={{0}: (8, {})} | custom-call | flops 4026531840 | bytes 7864320 | tf_op jit(solution)/shard_map/pallas_call | solution.py:271
  137.7 9.6 %shard_map.71 = (bf16[32,10,128,256]{3,2,1,0:T(8,128)(2,1)}, f32[10,32,128]{2,1,0:T(8,128)S(1)}, bf16[10,128,256]{2,1,0:T(8,128)(2,1)S(1)}, bf16[4,128,256]{2,1,0:T(8,128)(2,1)S(1)}) custom-call(s32[32]{0:T(128)} %fusion.3.s_hbm, s32[32,128]{1,0:T(8,128)S(1)} %broadcast_in_dim.17.cut_ref, ...), custom_call_target="tpu_custom_call", output_to_operand_aliasing={{0}: (8, {})} | custom-call | flops 4697620480 | bytes 9175040 | tf_op jit(solution)/shard_map/pallas_call | solution.py:271
  147.4 0.0 copy-start.2
  147.4 5.9 %shard_map.72 = (bf16[32,10,128,256]{3,2,1,0:T(8,128)(2,1)}, f32[10,32,128]{2,1,0:T(8,128)S(1)}, bf16[10,128,256]{2,1,0:T(8,128)(2,1)S(1)}, bf16[4,128,256]{2,1,0:T(8,128)(2,1)S(1)}) custom-call(s32[32]{0:T(128)} %fusion.3.s_hbm, s32[32,128]{1,0:T(8,128)S(1)} %broadcast_in_dim.17.cut_ref, ...), custom_call_target="tpu_custom_call", output_to_operand_aliasing={{0}: (8, {})} | custom-call | flops 2684354560 | bytes 5242880 | tf_op jit(solution)/shard_map/pallas_call | solution.py:271
  153.2 0.0 copy-done.2
  153.3 0.0 copy-start.5
  153.3 4.5 %shard_map.73 = (bf16[32,10,128,256]{3,2,1,0:T(8,128)(2,1)}, f32[10,32,128]{2,1,0:T(8,128)S(1)}, bf16[10,128,256]{2,1,0:T(8,128)(2,1)S(1)}, bf16[4,128,256]{2,1,0:T(8,128)(2,1)S(1)}) custom-call(s32[32]{0:T(128)} %fusion.3.s_hbm, s32[32,128]{1,0:T(8,128)S(1)} %broadcast_in_dim.17.cut_ref, ...), custom_call_target="tpu_custom_call", output_to_operand_aliasing={{0}: (8, {})} | custom-call | flops 2013265920 | bytes 3932160 | tf_op jit(solution)/shard_map/pallas_call | solution.py:271
  157.8 0.0 copy-done.5
  157.8 3.6 %shard_map.74 = (bf16[32,10,128,256]{3,2,1,0:T(8,128)(2,1)}, f32[10,32,128]{2,1,0:T(8,128)}) custom-call(s32[32]{0:T(128)} %fusion.3.s_hbm, s32[32,128]{1,0:T(8,128)S(1)} %broadcast_in_dim.17.cut_ref, bf16[32,10,128,256]{3,2,1,0:T(8,128)(2,1)} %bitcast.9, bf16[32,128,256]{2,1,0:T(8,128)(2,1)} %k_ref.17, ...), custom_call_target="tpu_custom_call", output_to_operand_aliasing={{0}: (8, {})} | custom-call | flops 1342177280 | bytes 2621440 | tf_op jit(solution)/shard_map/pallas_call | solution.py:271
  (2 shorter events, 0.0 us)
Async XLA Ops:
  6.8 105.2 %collective-permute-start = (bf16[8208,256]{1,0:T(8,128)(2,1)}, bf16[8208,256]{1,0:T(8,128)(2,1)}, u32[]{:S(2)}, u32[]{:S(2)}) collective-permute-start(bf16[8208,256]{1,0:T(8,128)(2,1)} %get-tuple-element.35), channel_id=1, source_target_pairs={{0,1},{2,3},{4,5},{6,7}} | collective-permute-start | bytes 12607496 | tf_op jit(solution)/shard_map/ppermute | solution.py:333
  8.1 28.3 %collective-permute-start.3 = (bf16[768,256]{1,0:T(8,128)(2,1)S(1)}, bf16[768,256]{1,0:T(8,128)(2,1)S(1)}, u32[]{:S(2)}, u32[]{:S(2)}) collective-permute-start(bf16[768,256]{1,0:T(8,128)(2,1)S(1)} %get-tuple-element.37), channel_id=1, source_target_pairs={{0,2},{1,3},{4,6},{5,7}} | collective-permute-start | bytes 1179656 | tf_op jit(solution)/shard_map/ppermute | solution.py:333
  9.4 29.2 %collective-permute-start.4 = (bf16[1024,256]{1,0:T(8,128)(2,1)S(1)}, bf16[1024,256]{1,0:T(8,128)(2,1)S(1)}, u32[]{:S(2)}, u32[]{:S(2)}) collective-permute-start(bf16[1024,256]{1,0:T(8,128)(2,1)S(1)} %get-tuple-element.38), channel_id=1, source_target_pairs={{0,2},{1,3},{4,6},{5,7}} | collective-permute-start | bytes 1572872 | tf_op jit(solution)/shard_map/ppermute | solution.py:333
  10.7 23.8 %collective-permute-start.2 = (bf16[512,256]{1,0:T(8,128)(2,1)S(1)}, bf16[512,256]{1,0:T(8,128)(2,1)S(1)}, u32[]{:S(2)}, u32[]{:S(2)}) collective-permute-start(bf16[512,256]{1,0:T(8,128)(2,1)S(1)} %get-tuple-element.36), channel_id=1, source_target_pairs={{0,2},{1,3},{4,6},{5,7}} | collective-permute-start | bytes 786440 | tf_op jit(solution)/shard_map/ppermute | solution.py:333
  12.0 97.5 %collective-permute-start.5 = (bf16[1792,256]{1,0:T(8,128)(2,1)}, bf16[1792,256]{1,0:T(8,128)(2,1)S(1)}, u32[]{:S(2)}, u32[]{:S(2)}) collective-permute-start(bf16[1792,256]{1,0:T(8,128)(2,1)} %get-tuple-element.39), channel_id=1, source_target_pairs={{0,2},{1,3},{4,6},{5,7}} | collective-permute-start | bytes 2752520 | tf_op jit(solution)/shard_map/ppermute | solution.py:333
  34.5 0.7 copy-start.3
  35.2 69.7 %collective-permute-start.7 = (bf16[1536,256]{1,0:T(8,128)(2,1)}, bf16[1536,256]{1,0:T(8,128)(2,1)S(1)}, u32[]{:S(2)}, u32[]{:S(2)}) collective-permute-start(bf16[1536,256]{1,0:T(8,128)(2,1)} %get-tuple-element.41), channel_id=1, source_target_pairs={{0,2},{1,3},{4,6},{5,7}} | collective-permute-start | bytes 2359304 | tf_op jit(solution)/shard_map/ppermute | solution.py:333
  36.5 2.1 %copy-start = (bf16[768,256]{1,0:T(8,128)(2,1)}, bf16[768,256]{1,0:T(8,128)(2,1)S(1)}, u32[]{:S(2)}) copy-start(bf16[768,256]{1,0:T(8,128)(2,1)S(1)} %collective-permute-done.3.mine_ref.fara_ref) | copy-start | bytes 1179652
  36.5 70.7 %collective-permute-start.6 = (bf16[1536,256]{1,0:T(8,128)(2,1)}, bf16[1536,256]{1,0:T(8,128)(2,1)S(1)}, u32[]{:S(2)}, u32[]{:S(2)}) collective-permute-start(bf16[1536,256]{1,0:T(8,128)(2,1)} %get-tuple-element.40), channel_id=1, source_target_pairs={{0,2},{1,3},{4,6},{5,7}} | collective-permute-start | bytes 2359304 | tf_op jit(solution)/shard_map/ppermute | solution.py:333
  38.7 60.6 %collective-permute-start.1 = (bf16[1040,256]{1,0:T(8,128)(2,1)}, bf16[1040,256]{1,0:T(8,128)(2,1)S(1)}, u32[]{:S(2)}, u32[]{:S(2)}) collective-permute-start(bf16[1040,256]{1,0:T(8,128)(2,1)} %shard_map.60), channel_id=1, source_target_pairs={{0,2},{1,3},{4,6},{5,7}} | collective-permute-start | bytes 1597448 | tf_op jit(solution)/shard_map/ppermute | solution.py:333
  40.8 1.0 copy-start.4
  50.4 1.0 copy-start.1
  147.4 5.9 %copy-start.2 = (bf16[768,256]{1,0:T(8,128)(2,1)S(1)}, bf16[768,256]{1,0:T(8,128)(2,1)}, u32[]{:S(2)}) copy-start(bf16[768,256]{1,0:T(8,128)(2,1)} %copy-done) | copy-start | bytes 1179652
  153.3 4.5 %copy-start.5 = (bf16[512,256]{1,0:T(8,128)(2,1)S(1)}, bf16[512,256]{1,0:T(8,128)(2,1)}, u32[]{:S(2)}) copy-start(bf16[512,256]{1,0:T(8,128)(2,1)} %copy-done.3) | copy-start | bytes 786436

commit v7 on v6

--- a/solution.py
+++ b/solution.py
@@ -8,7 +8,7 @@
 from jax.sharding import PartitionSpec as P
 
 
-CHUNKS = (4, 6, 6, 7, 4, 3, 2)
+CHUNKS = (4, 6, 6, 5, 4, 4, 3)
 BOUNDS = tuple(sum(CHUNKS[:n]) for n in range(len(CHUNKS) + 1))
 GROUP = 2
 DEPTH = 3
@@ -79,7 +79,7 @@
         _, lse_in, q_in, kv_in, *rest = rest
     o_ref, lse_ref, *rest = rest
     if last:
-        lse_out, (lse_ref, lse_sem, *rest) = lse_ref, rest
+        lse_out, (lse_ref, lse_sem, early_sem, *rest) = lse_ref, rest
     else:
         q_out, kv_out, *rest = rest
     s_ref, n_ref, q_buf, k_buf, v_buf, o_buf, s_sem, kv_sem, q_sem, o_sem, ahead_sem = rest
@@ -191,6 +191,11 @@
             buf[0, there] = kv_in[2 * half + 1]
         lse_ref[...] = lse_in[...]
 
+    if last:
+        ready = base // 8 * 8
+        early = pltpu.make_async_copy(lse_in.at[:, pl.ds(0, ready)], lse_out.at[:, pl.ds(0, ready)], early_sem)
+        early.start()
+
     @pl.loop(0, size)
     def _(step):
         @pl.when((step > 0) | first)
@@ -234,8 +239,10 @@
         n_ref[0] = s_ref[jnp.minimum(base + step + 1, batch - 1)]
 
     if last:
-        log_store = pltpu.make_async_copy(lse_ref, lse_out, lse_sem)
+        late = pl.ds(ready, batch - ready)
+        log_store = pltpu.make_async_copy(lse_ref.at[:, late], lse_out.at[:, late], lse_sem)
         log_store.start()
+        early.wait()
         log_store.wait()
     else:
         for copy in aheads():
@@ -272,7 +279,7 @@
         functools.partial(attend_kernel, first, last, base, size),
         in_specs=in_specs,
         out_specs=[hbm, hbm] if last else [hbm] + [vmem] * 3,
-        scratch_shapes=([pltpu.VMEM(out_shape[1].shape, jnp.float32), pltpu.SemaphoreType.DMA] if last else []) + [
+        scratch_shapes=([pltpu.VMEM(out_shape[1].shape, jnp.float32)] + [pltpu.SemaphoreType.DMA] * 2 if last else []) + [
             pltpu.SMEM(needs.shape, jnp.int32),
             pltpu.SMEM((1,), jnp.int32),
             pltpu.VMEM((DEPTH, heads, piece, head), jnp.bfloat16),

time: 163 us -> 162 us (level)
  transfers between devices with their start and end apart: 8 -> 8, of which waited for: 2 -> 3; matrix products, arithmetic and copies ran while one was open for 1% -> 1% of each run, Pallas kernels for 16% -> 16%
where the time goes in v7:
time: 162 us; the launch traced here: 161 us
  Pallas kernels  79.2 us (49%)
  waiting for transfers between devices  64.1 us (40%)
  starting transfers between devices  10.3 us (6%)
  local copies, waits for them, and re-layouts  5.4 us (3%)
    ppermute x8, waiting for transfers between devices, shift(): return lax.ppermute(x, 'cp', pairs)  64.1 us
    pallas_call x7, Pallas kernels, attend(): pl.pallas_call(functools.partial(attend_kernel, first, last, base, size),...  47.3 us
    pallas_call x7, Pallas kernels, swap(): pl.pallas_call(swap_kernel, in_specs=[vmem], out_specs=vmem, out_shape=ja...  24.9 us
    ppermute x8, starting transfers between devices, shift(): return lax.ppermute(x, 'cp', pairs)  10.3 us
    pallas_call x2, Pallas kernels, pack(): pl.pallas_call(functools.partial(pack_kernel, senders, ranges, tails), in...  6.93 us
    unnamed x12, local copies, waits for them, and re-layouts  3.59 us
  transfers between devices with their start and end apart: 8, of which 3 were waited for; matrix products, arithmetic and copies ran while one was open for 1% of the time, Pallas kernels for 16%

profile of v7, /device:TPU:7, one launch (start us, length us, event | category | flops | bytes accessed | tf_op | source)
XLA Modules:
  0.0 160.8 jit_solution(11651062937581868100)
XLA Ops:
  0.6 6.1 %shard_map.59 = (bf16[1536,256]{1,0:T(8,128)(2,1)}, bf16[1536,256]{1,0:T(8,128)(2,1)}, bf16[1280,256]{1,0:T(8,128)(2,1)}, bf16[1024,256]{1,0:T(8,128)(2,1)S(1)},...) custom-call(s32[32,128]{1,0:T(8,128)} %seg_ref.3, ...), custom_call_target="tpu_custom_call" | custom-call | flops 1048576 | bytes 4194304 | tf_op jit(solution)/shard_map/pallas_call | solution.py:66
  6.8 1.3 collective-permute-start
  8.1 1.3 collective-permute-start.4
  9.4 1.3 collective-permute-start.2
  10.7 1.3 collective-permute-start.3
  12.0 1.3 collective-permute-start.7
  13.3 15.5 %collective-permute-done.2.mine_ref.fara_ref = bf16[768,256]{1,0:T(8,128)(2,1)S(1)} collective-permute-done((bf16[768,256]{1,0:T(8,128)(2,1)S(1)}, bf16[768,256]{1,0:T(8,128)(2,1)S(1)}, u32[]{:S(2)}, u32[]{:S(2)}) %collective-permute-start.2) | collective-permute-done | bytes 393248 | tf_op jit(solution)/shard_map/ppermute | solution.py:340
  28.8 0.7 copy-done.3
  29.6 1.3 collective-permute-start.6
  30.8 0.0 collective-permute-done.4.mine_ref.fara_ref
  30.8 0.0 copy-start
  30.9 0.8 copy-done
  31.7 1.3 collective-permute-start.5
  32.9 0.8 shard_map.60
  33.8 6.3 %collective-permute-done.3.mine_ref.fara_ref = bf16[1024,256]{1,0:T(8,128)(2,1)S(1)} collective-permute-done((bf16[1024,256]{1,0:T(8,128)(2,1)S(1)}, bf16[1024,256]{1,0:T(8,128)(2,1)S(1)}, u32[]{:S(2)}, u32[]{:S(2)}) %collective-permute-start.3) | collective-permute-done | bytes 524320 | tf_op jit(solution)/shard_map/ppermute | solution.py:340
  40.0 1.3 collective-permute-start.1
  41.3 0.8 slice_reduce_fusion.7
  42.2 1.0 copy-done.4
  43.2 8.8 %shard_map.62.farb_ref = bf16[768,256]{1,0:T(8,128)(2,1)S(1)} custom-call(bf16[768,256]{1,0:T(8,128)(2,1)S(1)} %copy-done.4), custom_call_target="tpu_custom_call" | custom-call | flops 1048576 | bytes 786432 | tf_op jit(solution)/shard_map/pallas_call | solution.py:326
  52.0 0.0 copy-start.1
  52.0 1.0 copy-done.1
  53.0 1.9 %shard_map.64.farb_ref = bf16[1024,256]{1,0:T(8,128)(2,1)S(1)} custom-call(bf16[1024,256]{1,0:T(8,128)(2,1)S(1)} %copy-done.1), custom_call_target="tpu_custom_call" | custom-call | flops 1048576 | bytes 1048576 | tf_op jit(solution)/shard_map/pallas_call | solution.py:326
  54.9 1.9 %shard_map.63.farb_ref = bf16[1024,256]{1,0:T(8,128)(2,1)S(1)} custom-call(bf16[1024,256]{1,0:T(8,128)(2,1)S(1)} %collective-permute-done.3.mine_ref.fara_ref), custom_call_target="tpu_custom_call" | custom-call | flops 1048576 | bytes 1048576 | tf_op jit(solution)/shard_map/pallas_call | solution.py:326
  56.9 42.3 %collective-permute-done.1.mine_ref.fara_ref = bf16[1040,256]{1,0:T(8,128)(2,1)S(1)} collective-permute-done((bf16[1040,256]{1,0:T(8,128)(2,1)}, bf16[1040,256]{1,0:T(8,128)(2,1)S(1)}, u32[]{:S(2)}, u32[]{:S(2)}) %collective-permute-start.1) | collective-permute-done | bytes 532512 | tf_op jit(solution)/shard_map/ppermute | solution.py:340
  99.2 5.5 %shard_map.61.farb_ref = bf16[1040,256]{1,0:T(8,128)(2,1)S(1)} custom-call(bf16[1040,256]{1,0:T(8,128)(2,1)S(1)} %collective-permute-done.1.mine_ref.fara_ref), custom_call_target="tpu_custom_call" | custom-call | flops 1048576 | bytes 1064960 | tf_op jit(solution)/shard_map/pallas_call | solution.py:326
  104.7 0.1 slice_reduce_fusion.1
  104.8 0.0 collective-permute-done.5.mine_ref.fara_ref
  104.8 2.1 %shard_map.65.farb_ref = bf16[1280,256]{1,0:T(8,128)(2,1)S(1)} custom-call(bf16[1280,256]{1,0:T(8,128)(2,1)S(1)} %collective-permute-done.5.mine_ref.fara_ref), custom_call_target="tpu_custom_call" | custom-call | flops 1048576 | bytes 1310720 | tf_op jit(solution)/shard_map/pallas_call | solution.py:326
  107.0 0.0 collective-permute-done.7.mine_ref.fara_ref
  107.0 2.3 %shard_map.67.farb_ref = bf16[1536,256]{1,0:T(8,128)(2,1)S(1)} custom-call(bf16[1536,256]{1,0:T(8,128)(2,1)S(1)} %collective-permute-done.7.mine_ref.fara_ref), custom_call_target="tpu_custom_call" | custom-call | flops 1048576 | bytes 1572864 | tf_op jit(solution)/shard_map/pallas_call | solution.py:326
  109.3 0.0 collective-permute-done.6.mine_ref.fara_ref
  109.3 2.3 %shard_map.66.farb_ref = bf16[1536,256]{1,0:T(8,128)(2,1)S(1)} custom-call(bf16[1536,256]{1,0:T(8,128)(2,1)S(1)} %collective-permute-done.6.mine_ref.fara_ref), custom_call_target="tpu_custom_call" | custom-call | flops 1048576 | bytes 1572864 | tf_op jit(solution)/shard_map/pallas_call | solution.py:326
  111.6 0.0 collective-permute-done.near_ref
  111.6 0.8 slice_reduce_fusion.3
  112.4 0.1 broadcast_subtract_fusion
  112.5 0.6 fusion.3.s_hbm
  113.1 0.1 broadcast_in_dim.17.cut_ref
  113.2 7.2 %shard_map.68 = (bf16[32,10,128,256]{3,2,1,0:T(8,128)(2,1)}, f32[10,32,128]{2,1,0:T(8,128)S(1)}, bf16[10,128,256]{2,1,0:T(8,128)(2,1)S(1)}, bf16[4,128,256]{2,1,0:T(8,128)(2,1)S(1)}) custom-call(s32[32]{0:T(128)} %fusion.3.s_hbm, s32[32,128]{1,0:T(8,128)S(1)} %broadcast_in_dim.17.cut_ref, bf16[32,10,128,256]{3,2,1,0:T(8,128)(2,1)} %bitcast.3, ...), custom_call_target="tpu_custom_call" | custom-call | flops 2684354560 | bytes 5242880 | tf_op jit(solution)/shard_map/pallas_call | solution.py:278
  120.4 8.9 %shard_map.69 = (bf16[32,10,128,256]{3,2,1,0:T(8,128)(2,1)}, f32[10,32,128]{2,1,0:T(8,128)S(1)}, bf16[10,128,256]{2,1,0:T(8,128)(2,1)S(1)}, bf16[4,128,256]{2,1,0:T(8,128)(2,1)S(1)}) custom-call(s32[32]{0:T(128)} %fusion.3.s_hbm, s32[32,128]{1,0:T(8,128)S(1)} %broadcast_in_dim.17.cut_ref, ...), custom_call_target="tpu_custom_call", output_to_operand_aliasing={{0}: (8, {})} | custom-call | flops 4026531840 | bytes 7864320 | tf_op jit(solution)/shard_map/pallas_call | solution.py:278
  129.3 8.0 %shard_map.70 = (bf16[32,10,128,256]{3,2,1,0:T(8,128)(2,1)}, f32[10,32,128]{2,1,0:T(8,128)S(1)}, bf16[10,128,256]{2,1,0:T(8,128)(2,1)S(1)}, bf16[4,128,256]{2,1,0:T(8,128)(2,1)S(1)}) custom-call(s32[32]{0:T(128)} %fusion.3.s_hbm, s32[32,128]{1,0:T(8,128)S(1)} %broadcast_in_dim.17.cut_ref, ...), custom_call_target="tpu_custom_call", output_to_operand_aliasing={{0}: (8, {})} | custom-call | flops 4026531840 | bytes 7864320 | tf_op jit(solution)/shard_map/pallas_call | solution.py:278
  137.3 0.0 copy-start.2
  137.3 7.2 %shard_map.71 = (bf16[32,10,128,256]{3,2,1,0:T(8,128)(2,1)}, f32[10,32,128]{2,1,0:T(8,128)S(1)}, bf16[10,128,256]{2,1,0:T(8,128)(2,1)S(1)}, bf16[4,128,256]{2,1,0:T(8,128)(2,1)S(1)}) custom-call(s32[32]{0:T(128)} %fusion.3.s_hbm, s32[32,128]{1,0:T(8,128)S(1)} %broadcast_in_dim.17.cut_ref, ...), custom_call_target="tpu_custom_call", output_to_operand_aliasing={{0}: (8, {})} | custom-call | flops 3355443200 | bytes 6553600 | tf_op jit(solution)/shard_map/pallas_call | solution.py:278
  144.5 0.0 copy-done.2
  144.5 6.2 %shard_map.72 = (bf16[32,10,128,256]{3,2,1,0:T(8,128)(2,1)}, f32[10,32,128]{2,1,0:T(8,128)S(1)}, bf16[10,128,256]{2,1,0:T(8,128)(2,1)S(1)}, bf16[4,128,256]{2,1,0:T(8,128)(2,1)S(1)}) custom-call(s32[32]{0:T(128)} %fusion.3.s_hbm, s32[32,128]{1,0:T(8,128)S(1)} %broadcast_in_dim.17.cut_ref, ...), custom_call_target="tpu_custom_call", output_to_operand_aliasing={{0}: (8, {})} | custom-call | flops 2684354560 | bytes 5242880 | tf_op jit(solution)/shard_map/pallas_call | solution.py:278
  150.7 0.0 copy-start.5
  150.7 5.4 %shard_map.73 = (bf16[32,10,128,256]{3,2,1,0:T(8,128)(2,1)}, f32[10,32,128]{2,1,0:T(8,128)S(1)}, bf16[10,128,256]{2,1,0:T(8,128)(2,1)S(1)}, bf16[4,128,256]{2,1,0:T(8,128)(2,1)S(1)}) custom-call(s32[32]{0:T(128)} %fusion.3.s_hbm, s32[32,128]{1,0:T(8,128)S(1)} %broadcast_in_dim.17.cut_ref, ...), custom_call_target="tpu_custom_call", output_to_operand_aliasing={{0}: (8, {})} | custom-call | flops 2684354560 | bytes 5242880 | tf_op jit(solution)/shard_map/pallas_call | solution.py:278
  156.2 0.0 copy-done.5
  156.2 4.4 %shard_map.74 = (bf16[32,10,128,256]{3,2,1,0:T(8,128)(2,1)}, f32[10,32,128]{2,1,0:T(8,128)}) custom-call(s32[32]{0:T(128)} %fusion.3.s_hbm, s32[32,128]{1,0:T(8,128)S(1)} %broadcast_in_dim.17.cut_ref, bf16[32,10,128,256]{3,2,1,0:T(8,128)(2,1)} %bitcast.9, bf16[32,128,256]{2,1,0:T(8,128)(2,1)} %k_ref.17, ...), custom_call_target="tpu_custom_call", output_to_operand_aliasing={{0}: (8, {})} | custom-call | flops 2013265920 | bytes 3932160 | tf_op jit(solution)/shard_map/pallas_call | solution.py:278
  (2 shorter events, 0.0 us)
Async XLA Ops:
  6.8 104.9 %collective-permute-start = (bf16[8208,256]{1,0:T(8,128)(2,1)}, bf16[8208,256]{1,0:T(8,128)(2,1)}, u32[]{:S(2)}, u32[]{:S(2)}) collective-permute-start(bf16[8208,256]{1,0:T(8,128)(2,1)} %get-tuple-element.35), channel_id=1, source_target_pairs={{0,1},{2,3},{4,5},{6,7}} | collective-permute-start | bytes 12607496 | tf_op jit(solution)/shard_map/ppermute | solution.py:340
  8.1 22.8 %collective-permute-start.4 = (bf16[1024,256]{1,0:T(8,128)(2,1)S(1)}, bf16[1024,256]{1,0:T(8,128)(2,1)S(1)}, u32[]{:S(2)}, u32[]{:S(2)}) collective-permute-start(bf16[1024,256]{1,0:T(8,128)(2,1)S(1)} %get-tuple-element.38), channel_id=1, source_target_pairs={{0,2},{1,3},{4,6},{5,7}} | collective-permute-start | bytes 1572872 | tf_op jit(solution)/shard_map/ppermute | solution.py:340
  9.4 19.4 %collective-permute-start.2 = (bf16[768,256]{1,0:T(8,128)(2,1)S(1)}, bf16[768,256]{1,0:T(8,128)(2,1)S(1)}, u32[]{:S(2)}, u32[]{:S(2)}) collective-permute-start(bf16[768,256]{1,0:T(8,128)(2,1)S(1)} %get-tuple-element.36), channel_id=1, source_target_pairs={{0,2},{1,3},{4,6},{5,7}} | collective-permute-start | bytes 1179656 | tf_op jit(solution)/shard_map/ppermute | solution.py:340
  10.7 29.4 %collective-permute-start.3 = (bf16[1024,256]{1,0:T(8,128)(2,1)S(1)}, bf16[1024,256]{1,0:T(8,128)(2,1)S(1)}, u32[]{:S(2)}, u32[]{:S(2)}) collective-permute-start(bf16[1024,256]{1,0:T(8,128)(2,1)S(1)} %get-tuple-element.37), channel_id=1, source_target_pairs={{0,2},{1,3},{4,6},{5,7}} | collective-permute-start | bytes 1572872 | tf_op jit(solution)/shard_map/ppermute | solution.py:340
  12.0 95.0 %collective-permute-start.7 = (bf16[1536,256]{1,0:T(8,128)(2,1)}, bf16[1536,256]{1,0:T(8,128)(2,1)S(1)}, u32[]{:S(2)}, u32[]{:S(2)}) collective-permute-start(bf16[1536,256]{1,0:T(8,128)(2,1)} %get-tuple-element.41), channel_id=1, source_target_pairs={{0,2},{1,3},{4,6},{5,7}} | collective-permute-start | bytes 2359304 | tf_op jit(solution)/shard_map/ppermute | solution.py:340
  28.8 0.7 copy-start.3
  29.6 79.7 %collective-permute-start.6 = (bf16[1536,256]{1,0:T(8,128)(2,1)}, bf16[1536,256]{1,0:T(8,128)(2,1)S(1)}, u32[]{:S(2)}, u32[]{:S(2)}) collective-permute-start(bf16[1536,256]{1,0:T(8,128)(2,1)} %get-tuple-element.40), channel_id=1, source_target_pairs={{0,2},{1,3},{4,6},{5,7}} | collective-permute-start | bytes 2359304 | tf_op jit(solution)/shard_map/ppermute | solution.py:340
  30.8 0.8 copy-start
  31.7 73.1 %collective-permute-start.5 = (bf16[1280,256]{1,0:T(8,128)(2,1)}, bf16[1280,256]{1,0:T(8,128)(2,1)S(1)}, u32[]{:S(2)}, u32[]{:S(2)}) collective-permute-start(bf16[1280,256]{1,0:T(8,128)(2,1)} %get-tuple-element.39), channel_id=1, source_target_pairs={{0,2},{1,3},{4,6},{5,7}} | collective-permute-start | bytes 1966088 | tf_op jit(solution)/shard_map/ppermute | solution.py:340
  40.0 59.2 %collective-permute-start.1 = (bf16[1040,256]{1,0:T(8,128)(2,1)}, bf16[1040,256]{1,0:T(8,128)(2,1)S(1)}, u32[]{:S(2)}, u32[]{:S(2)}) collective-permute-start(bf16[1040,256]{1,0:T(8,128)(2,1)} %shard_map.60), channel_id=1, source_target_pairs={{0,2},{1,3},{4,6},{5,7}} | collective-permute-start | bytes 1597448 | tf_op jit(solution)/shard_map/ppermute | solution.py:340
  42.2 1.0 copy-start.4
  52.0 1.0 copy-start.1
  137.3 7.3 %copy-start.2 = (bf16[1024,256]{1,0:T(8,128)(2,1)S(1)}, bf16[1024,256]{1,0:T(8,128)(2,1)}, u32[]{:S(2)}) copy-start(bf16[1024,256]{1,0:T(8,128)(2,1)} %copy-done) | copy-start | bytes 1572868
  150.7 5.4 %copy-start.5 = (bf16[768,256]{1,0:T(8,128)(2,1)S(1)}, bf16[768,256]{1,0:T(8,128)(2,1)}, u32[]{:S(2)}) copy-start(bf16[768,256]{1,0:T(8,128)(2,1)} %copy-done.3) | copy-start | bytes 1179652
